TPU v7x, 256 devices: a whole 4x4x8 slice. The times are simulated.
256 devices in a mesh: gx: 8 (over x, core), gy: 4 (over z_hi), gz: 8 (over y, z_lo).
Axes of the slice: x: 4, y: 4, z: 8 (z_hi: 4, z_lo: 2; z = z_hi * 2 + z_lo), core: 2. Of those that a mesh axis runs over, the one named last changes fastest.
Arguments:
- occupied: float32 [16, 32, 16, 1024], P(None, 'gx', 'gy', 'gz'), may hold values from -6 to 6
- virtual: float32 [16, 32, 16, 1024], P(None, 'gx', 'gy', 'gz'), may hold values from -6 to 6
- kernel_fields: float32 [4, 32, 16, 1024], P(None, 'gx', 'gy', 'gz'), may hold values from -1.5 to 1.5
- density_grad: float32 [3, 32, 16, 1024], P(None, 'gx', 'gy', 'gz'), may hold values from -6 to 6
Outputs:
- potential: float32 [256, 32, 16, 1024], P(None, 'gx', 'gy', 'gz')
- casida: float32 [256, 256], P(('gx', 'gy', 'gz'))
All inputs are finite; a program needn't handle non-finite values.
Results may differ from a plain program's by a relative error of at most 0.00013.
Values sent between devices are 32-bit elements; how exact they have to be, the bound alone decides.
A program may use at most 64 MiB of HBM per device.

v0:
```python
import jax
import jax.numpy as jnp
from jax import lax
from jax.sharding import Mesh
from jax.sharding import PartitionSpec as P

GX_GY_GZ = ("gx_0", "gx_1", "gy", "gz_0", "gz_1")
GX = ("gx_0", "gx_1")
GZ = ("gz_0", "gz_1")


def padded(block, sides, width):
    for axis, dim in sides:
        count = lax.axis_size(axis)
        forward = [(i, i + 1) for i in range(count - 1)]
        forward.append((count - 1, 0))
        backward = [(target, source) for source, target in forward]
        low = lax.ppermute(
            lax.slice_in_dim(block, block.shape[dim] - width, None, axis=dim), axis, forward
        )
        high = lax.ppermute(lax.slice_in_dim(block, 0, width, axis=dim), axis, backward)
        block = jnp.concatenate([low, block, high], axis=dim)
    return block


def split_up(value, dim, size):
    lengths = value.shape
    pieces = value.reshape(*lengths[:dim], size, lengths[dim] // size, *lengths[dim + 1 :])
    return jnp.moveaxis(pieces, dim, 0)


def piece_ends(length, count):
    hop = length // count
    if hop >= 8:
        hop -= hop % 8
    return [hop * k for k in range(1, count)]


def reduced_to_own(pieces, axes, order):
    inside = pieces.shape[1:]
    pieces = pieces.reshape(*(lax.axis_size(a) for a in axes), *inside)
    pieces = jnp.moveaxis(pieces, order, range(len(axes))).reshape(-1, *inside)
    for k in order:
        pieces = lax.psum_scatter(pieces, axes[k], scatter_dimension=0, tiled=True)
    return pieces[0]


def sum_at_once(value, axes, dim):
    pieces = split_up(value, dim, lax.axis_size(axes))
    widest = max(range(1, max(2, pieces.ndim - 1)), key=lambda d: pieces.shape[d])
    count, gathered = (len(axes), [])
    for first, share in enumerate(
        jnp.split(pieces, piece_ends(pieces.shape[widest], count), axis=widest)
    ):
        if share.size:
            order = [(first + k) % count for k in range(count)]
            gathered.append(reduced_to_own(share, axes, order))
    return jnp.concatenate(gathered, axis=widest - 1)


def window(values, offsets):
    starts = (0,) + tuple((2 + offsets[dimension] for dimension in range(3)))
    limits = (values.shape[0],) + tuple(
        (values.shape[dimension + 1] - 2 + offsets[dimension] for dimension in range(3))
    )
    return lax.slice(values, starts, limits)


def derivative(values, dimension):

    def shifted(offset):
        offsets = [0, 0, 0]
        offsets[dimension] = offset
        return window(values, offsets)

    inner_diff = shifted(1) - shifted(-1)
    outer_diff = shifted(2) - shifted(-2)
    return (8.0 * inner_diff - outer_diff) / 12.0


def trim_rim(values, margin):
    return values[:, margin:-margin, margin:-margin, margin:-margin]


def on_device(occupied, virtual, kernel_fields, density_grad):
    local_kernel = kernel_fields[0]
    mixed_kernel = kernel_fields[1]
    nvir = virtual.shape[0]
    occ_wide = padded(occupied, ((GX, 1), ("gy", 2), (GZ, 3)), 4)
    vir_wide = padded(virtual, ((GX, 1), ("gy", 2), (GZ, 3)), 4)
    stacked = jnp.concatenate([kernel_fields, density_grad], axis=0)
    field_wide = padded(stacked, ((GX, 1), ("gy", 2), (GZ, 3)), 2)

    def pair_block(scan_state, orbital):
        dens_wide = orbital[None] * vir_wide
        slopes = [derivative(dens_wide, dimension) for dimension in range(3)]
        dens_middle = trim_rim(dens_wide, 2)
        aligned = field_wide[4] * slopes[0] + field_wide[5] * slopes[1] + field_wide[6] * slopes[2]
        scalar = field_wide[1] * dens_middle + field_wide[2] * aligned
        fluxes = [
            scalar * field_wide[4 + dimension] + field_wide[3] * slopes[dimension]
            for dimension in range(3)
        ]
        divergence = derivative(fluxes[0], 0) + derivative(fluxes[1], 1) + derivative(fluxes[2], 2)
        return (
            scan_state,
            local_kernel * trim_rim(dens_middle, 2)
            + mixed_kernel * trim_rim(aligned, 2)
            - divergence,
        )

    unused_state, stacked_potential = lax.scan(pair_block, jnp.zeros((), jnp.float32), occ_wide)
    nocc = occupied.shape[0]
    cells = occupied.shape[1] * occupied.shape[2] * occupied.shape[3]
    potential = stacked_potential.reshape((nocc * nvir,) + occupied.shape[1:])
    devices_all = lax.axis_size(GX) * lax.axis_size("gy") * lax.axis_size(GZ)
    total_cells = cells * devices_all
    flat_potential = potential.reshape((nocc * nvir, cells))
    occ_flat = occupied.reshape((nocc, cells))
    vir_flat = virtual.reshape((nvir, cells))
    own_rows = nocc * nvir // devices_all
    pair_index = lax.iota(jnp.int32, own_rows * lax.axis_size(GX_GY_GZ))
    occ_pick = (pair_index[:, None] // nvir == lax.iota(jnp.int32, nocc)[None, :]).astype(
        jnp.float32
    )
    vir_pick = (pair_index[:, None] % nvir == lax.iota(jnp.int32, nvir)[None, :]).astype(
        jnp.float32
    )
    occ_rows = jnp.dot(
        occ_pick, occ_flat, precision=lax.Precision.HIGHEST, preferred_element_type=jnp.float32
    )
    vir_rows = jnp.dot(
        vir_pick, vir_flat, precision=lax.Precision.HIGHEST, preferred_element_type=jnp.float32
    )
    casida = sum_at_once(
        lax.dot_general(
            occ_rows * vir_rows,
            flat_potential,
            (((1,), (1,)), ((), ())),
            precision=lax.Precision.HIGHEST,
            preferred_element_type=jnp.float32,
        ),
        GX_GY_GZ,
        0,
    ) * (1.0 / total_cells)
    return (potential, casida)


def solution(mesh):
    torus = Mesh(
        mesh.devices.reshape(4, 2, mesh.shape["gy"], 4, 2), ("gx_0", "gx_1", "gy", "gz_0", "gz_1")
    )
    placed = (
        P(None, GX, "gy", GZ),
        P(None, GX, "gy", GZ),
        P(None, GX, "gy", GZ),
        P(None, GX, "gy", GZ),
    )
    return jax.shard_map(
        on_device,
        mesh=torus,
        in_specs=placed,
        out_specs=(P(None, GX, "gy", GZ), P(GX_GY_GZ, None)),
        check_vma=False,
    )
```

profile of v0, /device:TPU:1, one launch (start us, length us, event | category | flops | bytes accessed | tf_op | source)
XLA Modules:
  0.0 401.7 jit_solution(2092963522491438722)
XLA Ops:
  31.7 3.5 collective-permute-start.17
  38.6 5.6 %collective-permute-start.1 = (f32[16,4,4,128]{3,0,2,1:T(8,128)}, f32[16,4,4,128]{3,0,2,1:T(8,128)S(1)}, u32[]{:S(2)}, u32[]{:S(2)}) collective-permute-start(f32[16,4,4,128]{3,0,2,1:T(8,128)} %copy.18), channel_id=1, source_target_pairs={{32,0},{64,32},{96,64},{128,96},{160,128},{192,160},{224,192},{0,2... | collective-permute-start | bytes 393224 | tf_op jit(solution)/shard_map/ppermute | solution.py:21
  55.6 19.8 %collective-permute-done.8 = f32[16,12,4,128]{3,0,2,1:T(8,128)S(1)} collective-permute-done((f32[16,12,4,128]{3,0,2,1:T(8,128)S(1)}, f32[16,12,4,128]{3,0,2,1:T(8,128)S(1)}, u32[]{:S(2)}, u32[]{:S(2)}) %collective-permute-start.8) | collective-permute-done | bytes 393248 | tf_op jit(solution)/shard_map/ppermute | solution.py:18
  82.6 3.6 collective-permute-start.11
  91.3 3.6 collective-permute-start.5
  114.7 4.3 %pad_maximum_fusion = f32[16,12,12,136]{3,0,2,1:T(8,128)} fusion(f32[16,12,12,4]{3,0,2,1:T(8,128)} %copy.24, f32[16,12,4,128]{3,0,2,1:T(8,128)} %collective-permute-done.3, f32[16,12,4,128]{3,0,2,1:T(8,128)S(1)} %constant_dynamic-update-slice_fusion, f32[16,12,4,128]{3,0,2,1:T(8,128)} %collective-permute-done.2, f32[16,12,12,4]{3,0,2,1:T(8,128)} %copy.23), kind=kLoop, calls=%fused_computation.52 | loop fusion | flops 1253376 | bytes 2506752 | tf_op jit(solution)/shard_map/concatenate | solution.py:22
  118.9 150.3 %while.10 = (s32[]{:T(128)}, f32[16,16,4,4,128]{4,3,2,1,0:T(4,128)}, f32[1,4,4,128]{3,2,1,0:T(4,128)S(1)}, f32[16,12,12,136]{3,0,2,1:T(8,128)}, f32[16,12,12,136...) while((s32[]{:T(128)}, f32[16,16,4,4,128]{4,3,2,1,0:T(4,128)}, ...), condition=%wide.region_1.2_spmd, body=%wide.region_0.1_spmd.sunk | while | flops 5295106 | bytes 18330712 | solution.py:112
  122.7 3.4 multiply_add_fusion.7
  132.1 3.4 multiply_add_fusion.7
  141.5 3.4 multiply_add_fusion.7
  150.9 3.4 multiply_add_fusion.7
  160.3 3.4 multiply_add_fusion.7
  169.7 3.4 multiply_add_fusion.7
  179.1 3.4 multiply_add_fusion.7
  188.5 3.4 multiply_add_fusion.7
  197.9 3.4 multiply_add_fusion.7
  235.5 3.4 multiply_add_fusion.7
  244.9 3.4 multiply_add_fusion.7
  272.5 7.0 %fusion.22 = f32[2,4,2,4,4,1,256]{6,0,4,3,2,1,5:T(2,128)S(1)} fusion(f32[4,2,4,4,2,2048]{5,4,3,2,1,0:T(2,128)S(1)} %copy-done, f32[256,2048,1,1,1,1]{1,0,2,3,4,5:T(8,128)} %reshape.97), kind=kOutput, calls=%fused_computation.58 | convolution fusion | flops 1610612736 | bytes 4456448 | tf_op jit(solution)/shard_map/dot_general | solution.py:136
  281.8 32.7 %all-reduce.8.cloned.1.call-done = f32[256,1,256]{2,1,0:T(1,128)} async-done(((f32[256,1,256]{2,1,0:T(1,128)}), f32[256,1,256]{2,1,0:T(1,128)}) %all-reduce.8.cloned.1.call-update) | async-done | bytes 262160
  320.4 41.8 %all-reduce.10.cloned.1.call-done = f32[128,1,256]{2,1,0:T(1,128)} async-done(((f32[128,1,256]{2,1,0:T(1,128)}), f32[128,1,256]{2,1,0:T(1,128)}) %all-reduce.10.cloned.1.call-update) | async-done | bytes 131088
  362.9 6.0 %all-reduce.2 = f32[32,1,256]{2,1,0:T(1,128)S(1)} all-reduce(f32[32,1,256]{2,1,0:T(1,128)S(1)} %constant_dynamic-slice_fusion.4), channel_id=4, replica_groups=mesh['gx_0'=4,'gx_1'=2,'gy'=4,'gz_0'=4,'gz_1'=2] {'gx_1'}, use_global_device_ids=true, to_apply=%region_4.5.clone | all-reduce | flops 8192 | bytes 65536
  368.9 16.3 %all-reduce.3 = f32[16,1,256]{2,1,0:T(1,128)S(1)} all-reduce(f32[16,1,256]{2,1,0:T(1,128)S(1)} %constant_dynamic-slice_fusion.3), channel_id=5, replica_groups=mesh['gx_0'=4,'gx_1'=2,'gy'=4,'gz_0'=4,'gz_1'=2] {'gy'}, use_global_device_ids=true, to_apply=%region_5.6.clone | all-reduce | flops 4096 | bytes 32768
  385.2 8.4 %all-reduce.4 = f32[4,1,256]{2,1,0:T(1,128)S(1)} all-reduce(f32[4,1,256]{2,1,0:T(1,128)S(1)} %constant_dynamic-slice_fusion.2), channel_id=6, replica_groups=mesh['gx_0'=4,'gx_1'=2,'gy'=4,'gz_0'=4,'gz_1'=2] {'gz_0'}, use_global_device_ids=true, to_apply=%region_6.7.clone | all-reduce | flops 1024 | bytes 8192
  (223 shorter events, 193.8 us)
Async XLA Ops:
  7.2 307.3 %all-reduce.8.cloned.1.call-start = ((), (), s32[]{:S(2)}) async-start(), calls=%async_computation | async-start | bytes 524288
  8.8 36.6 %collective-permute-start.6 = (f32[16,4,4,128]{3,0,2,1:T(8,128)}, f32[16,4,4,128]{3,0,2,1:T(8,128)}, u32[]{:S(2)}, u32[]{:S(2)}) collective-permute-start(f32[16,4,4,128]{3,0,2,1:T(8,128)} %copy.25), channel_id=1, source_target_pairs={{0,32},{32,64},{64,96},{96,128},{128,160},{160,192},{192,224},{224... | collective-permute-start | bytes 393224 | tf_op jit(solution)/shard_map/ppermute | solution.py:18
  11.4 35.0 %collective-permute-start.7 = (f32[16,4,4,128]{3,0,2,1:T(8,128)}, f32[16,4,4,128]{3,0,2,1:T(8,128)}, u32[]{:S(2)}, u32[]{:S(2)}) collective-permute-start(f32[16,4,4,128]{3,0,2,1:T(8,128)} %copy.25), channel_id=1, source_target_pairs={{32,0},{64,32},{96,64},{128,96},{160,128},{192,160},{224,192},{0,2... | collective-permute-start | bytes 393224 | tf_op jit(solution)/shard_map/ppermute | solution.py:21
  13.6 8.0 %collective-permute-start.12 = (f32[7,2,4,128]{3,2,1,0:T(4,128)S(1)}, f32[7,2,4,128]{3,2,1,0:T(4,128)S(1)}, u32[]{:S(2)}, u32[]{:S(2)}) collective-permute-start(f32[7,2,4,128]{3,2,1,0:T(4,128)S(1)} %get-tuple-element.91), channel_id=1, source_target_pairs={{0,32},{32,64},{64,96},{96,128},{128,160},{160,192},{192,224},{224... | collective-permute-start | bytes 86024 | tf_op jit(solution)/shard_map/ppermute | solution.py:18
  14.7 6.8 %collective-permute-start.13 = (f32[7,2,4,128]{3,2,1,0:T(4,128)S(1)}, f32[7,2,4,128]{3,2,1,0:T(4,128)S(1)}, u32[]{:S(2)}, u32[]{:S(2)}) collective-permute-start(f32[7,2,4,128]{3,2,1,0:T(4,128)S(1)} %get-tuple-element.92), channel_id=1, source_target_pairs={{32,0},{64,32},{96,64},{128,96},{160,128},{192,160},{224,192},{0,2... | collective-permute-start | bytes 86024 | tf_op jit(solution)/shard_map/ppermute | solution.py:21
  18.1 32.8 %collective-permute-start = (f32[16,4,4,128]{3,0,2,1:T(8,128)}, f32[16,4,4,128]{3,0,2,1:T(8,128)}, u32[]{:S(2)}, u32[]{:S(2)}) collective-permute-start(f32[16,4,4,128]{3,0,2,1:T(8,128)} %copy.18), channel_id=1, source_target_pairs={{0,32},{32,64},{64,96},{96,128},{128,160},{160,192},{192,224},{224... | collective-permute-start | bytes 393224 | tf_op jit(solution)/shard_map/ppermute | solution.py:18
  21.6 8.7 %collective-permute-start.14 = (f32[7,8,2,128]{3,2,1,0:T(2,128)S(1)}, f32[7,8,2,128]{3,2,1,0:T(2,128)S(1)}, u32[]{:S(2)}, u32[]{:S(2)}) collective-permute-start(f32[7,8,2,128]{3,2,1,0:T(2,128)S(1)} %get-tuple-element.89), channel_id=1, source_target_pairs={{0,8},{8,16},{16,24},{24,0},{1,9},{9,17},{17,25},{25,1},{2,10},{10... | collective-permute-start | bytes 172040 | tf_op jit(solution)/shard_map/ppermute | solution.py:18
  24.6 6.7 %collective-permute-start.15 = (f32[7,8,2,128]{3,2,1,0:T(2,128)S(1)}, f32[7,8,2,128]{3,2,1,0:T(2,128)S(1)}, u32[]{:S(2)}, u32[]{:S(2)}) collective-permute-start(f32[7,8,2,128]{3,2,1,0:T(2,128)S(1)} %get-tuple-element.90), channel_id=1, source_target_pairs={{8,0},{16,8},{24,16},{0,24},{9,1},{17,9},{25,17},{1,25},{10,2},{18... | collective-permute-start | bytes 172040 | tf_op jit(solution)/shard_map/ppermute | solution.py:21
  31.5 7.1 %collective-permute-start.16 = (f32[7,8,8,2]{3,2,1,0:T(8,128)S(1)}, f32[7,8,8,2]{3,2,1,0:T(8,128)S(1)}, u32[]{:S(2)}, u32[]{:S(2)}) collective-permute-start(f32[7,8,8,2]{3,2,1,0:T(8,128)S(1)} %get-tuple-element.87), channel_id=1, source_target_pairs={{0,1},{1,2},{2,3},{3,4},{4,5},{5,6},{6,7},{7,0},{8,9},{9,10},{10,1... | collective-permute-start | bytes 10760 | tf_op jit(solution)/shard_map/ppermute | solution.py:18
  31.7 12.5 %collective-permute-start.17 = (f32[7,8,8,2]{3,2,1,0:T(8,128)S(1)}, f32[7,8,8,2]{3,2,1,0:T(8,128)S(1)}, u32[]{:S(2)}, u32[]{:S(2)}) collective-permute-start(f32[7,8,8,2]{3,2,1,0:T(8,128)S(1)} %get-tuple-element.88), channel_id=1, source_target_pairs={{1,0},{2,1},{3,2},{4,3},{5,4},{6,5},{7,6},{0,7},{9,8},{10,9},{11,1... | collective-permute-start | bytes 10760 | tf_op jit(solution)/shard_map/ppermute | solution.py:21
  38.6 13.4 %collective-permute-start.1 = (f32[16,4,4,128]{3,0,2,1:T(8,128)}, f32[16,4,4,128]{3,0,2,1:T(8,128)S(1)}, u32[]{:S(2)}, u32[]{:S(2)}) collective-permute-start(f32[16,4,4,128]{3,0,2,1:T(8,128)} %copy.18), channel_id=1, source_target_pairs={{32,0},{64,32},{96,64},{128,96},{160,128},{192,160},{224,192},{0,2... | collective-permute-start | bytes 393224 | tf_op jit(solution)/shard_map/ppermute | solution.py:21
  47.3 28.2 %collective-permute-start.8 = (f32[16,12,4,128]{3,0,2,1:T(8,128)S(1)}, f32[16,12,4,128]{3,0,2,1:T(8,128)S(1)}, u32[]{:S(2)}, u32[]{:S(2)}) collective-permute-start(f32[16,12,4,128]{3,0,2,1:T(8,128)S(1)} %constant_dynamic-update-slice_fusion.3), channel_id=1, source_target_pairs={{0,8},{8,16},{16,24},{24,0},{1,9},{9,17},{17,25},{25,1},{2,10},{10... | collective-permute-start | bytes 1179656 | tf_op jit(solution)/shard_map/ppermute | solution.py:18
  50.7 27.3 %collective-permute-start.9 = (f32[16,12,4,128]{3,0,2,1:T(8,128)S(1)}, f32[16,12,4,128]{3,0,2,1:T(8,128)S(1)}, u32[]{:S(2)}, u32[]{:S(2)}) collective-permute-start(f32[16,12,4,128]{3,0,2,1:T(8,128)S(1)} %constant_dynamic-update-slice_fusion.3), channel_id=1, source_target_pairs={{8,0},{16,8},{24,16},{0,24},{9,1},{17,9},{25,17},{1,25},{10,2},{18... | collective-permute-start | bytes 1179656 | tf_op jit(solution)/shard_map/ppermute | solution.py:21
  52.0 34.1 %collective-permute-start.2 = (f32[16,12,4,128]{3,0,2,1:T(8,128)S(1)}, f32[16,12,4,128]{3,0,2,1:T(8,128)}, u32[]{:S(2)}, u32[]{:S(2)}) collective-permute-start(f32[16,12,4,128]{3,0,2,1:T(8,128)S(1)} %constant_dynamic-update-slice_fusion), channel_id=1, source_target_pairs={{0,8},{8,16},{16,24},{24,0},{1,9},{9,17},{17,25},{25,1},{2,10},{10... | collective-permute-start | bytes 1179656 | tf_op jit(solution)/shard_map/ppermute | solution.py:18
  54.1 32.4 %collective-permute-start.3 = (f32[16,12,4,128]{3,0,2,1:T(8,128)S(1)}, f32[16,12,4,128]{3,0,2,1:T(8,128)}, u32[]{:S(2)}, u32[]{:S(2)}) collective-permute-start(f32[16,12,4,128]{3,0,2,1:T(8,128)S(1)} %constant_dynamic-update-slice_fusion), channel_id=1, source_target_pairs={{8,0},{16,8},{24,16},{0,24},{9,1},{17,9},{25,17},{1,25},{10,2},{18... | collective-permute-start | bytes 1179656 | tf_op jit(solution)/shard_map/ppermute | solution.py:21
  80.9 14.0 %collective-permute-start.10 = (f32[16,12,12,4]{0,3,2,1:T(4,128)}, f32[16,12,12,4]{0,3,2,1:T(4,128)}, u32[]{:S(2)}, u32[]{:S(2)}) collective-permute-start(f32[16,12,12,4]{0,3,2,1:T(4,128)} %copy.39), channel_id=1, source_target_pairs={{0,1},{1,2},{2,3},{3,4},{4,5},{5,6},{6,7},{7,0},{8,9},{9,10},{10,1... | collective-permute-start | bytes 110600 | tf_op jit(solution)/shard_map/ppermute | solution.py:18
  82.6 16.5 %collective-permute-start.11 = (f32[16,12,12,4]{0,3,2,1:T(4,128)}, f32[16,12,12,4]{0,3,2,1:T(4,128)}, u32[]{:S(2)}, u32[]{:S(2)}) collective-permute-start(f32[16,12,12,4]{0,3,2,1:T(4,128)} %copy.40), channel_id=1, source_target_pairs={{1,0},{2,1},{3,2},{4,3},{5,4},{6,5},{7,6},{0,7},{9,8},{10,9},{11,1... | collective-permute-start | bytes 110600 | tf_op jit(solution)/shard_map/ppermute | solution.py:21
  89.7 17.7 %collective-permute-start.4 = (f32[16,12,12,4]{0,3,2,1:T(4,128)}, f32[16,12,12,4]{0,3,2,1:T(4,128)}, u32[]{:S(2)}, u32[]{:S(2)}) collective-permute-start(f32[16,12,12,4]{0,3,2,1:T(4,128)} %copy.37), channel_id=1, source_target_pairs={{0,1},{1,2},{2,3},{3,4},{4,5},{5,6},{6,7},{7,0},{8,9},{9,10},{10,1... | collective-permute-start | bytes 110600 | tf_op jit(solution)/shard_map/ppermute | solution.py:18
  91.3 20.4 %collective-permute-start.5 = (f32[16,12,12,4]{0,3,2,1:T(4,128)}, f32[16,12,12,4]{0,3,2,1:T(4,128)}, u32[]{:S(2)}, u32[]{:S(2)}) collective-permute-start(f32[16,12,12,4]{0,3,2,1:T(4,128)} %copy.38), channel_id=1, source_target_pairs={{1,0},{2,1},{3,2},{4,3},{5,4},{6,5},{7,6},{0,7},{9,8},{10,9},{11,1... | collective-permute-start | bytes 110600 | tf_op jit(solution)/shard_map/ppermute | solution.py:21
  272.4 43.7 %copy-start.8 = (u32[256]{0:T(256)S(1)}, u32[256]{0:T(256)}, u32[]{:S(2)}) copy-start(u32[256]{0:T(256)} %constant.67) | copy-start | bytes 3076
  272.4 44.3 %copy-start.7 = (u32[256]{0:T(256)S(1)}, u32[256]{0:T(256)}, u32[]{:S(2)}) copy-start(u32[256]{0:T(256)} %constant.71) | copy-start | bytes 3076
  272.4 44.8 %copy-start.6 = (u32[256]{0:T(256)S(1)}, u32[256]{0:T(256)}, u32[]{:S(2)}) copy-start(u32[256]{0:T(256)} %constant.75) | copy-start | bytes 3076
  272.5 45.5 %copy-start.5 = (u32[256]{0:T(256)S(1)}, u32[256]{0:T(256)}, u32[]{:S(2)}) copy-start(u32[256]{0:T(256)} %constant.79) | copy-start | bytes 3076
  280.5 81.7 %all-reduce.10.cloned.1.call-start = ((), (), s32[]{:S(2)}) async-start(), calls=%async_computation.1 | async-start | bytes 262144
  (6 other events, 51.5 us)
Sparse Core Ops, SparseCore 0:
  280.6 33.8 all-reduce.7
  316.8 45.3 all-reduce.9
where the time goes:
time: 408 us; the launch traced here: 402 us
  other arithmetic  137 us (34%)
  waiting for transfers between devices  106 us (26%)
  local copies, waits for them, and re-layouts  62 us (15%)
  starting transfers between devices  36.1 us (9%)
  blocking collectives  30.7 us (8%)
  between operations  16.9 us (4%)
  matrix products  12 us (3%)
    unnamed x4, waiting for transfers between devices  74.5 us
    add x32, other arithmetic, pair_block(): scalar * field_wide[4 + dimension] + field_wide[3] * slopes[dimension]  62.8 us
    unnamed x3, blocking collectives  30.7 us
    dynamic_update_slice x16, other arithmetic, on_device(): lax.scan(pair_block, jnp.zeros((), jnp.float32), occ_wide)  26.2 us
    ppermute x9, waiting for transfers between devices, padded(): lax.ppermute(lax.slice_in_dim(block, block.shape[dim] - width, None, axis...  24 us
    ppermute x9, starting transfers between devices, padded(): lax.ppermute(lax.slice_in_dim(block, 0, width, axis=dim), axis, backward)  23.6 us
    dynamic_slice x32, local copies, waits for them, and re-layouts, on_device(): lax.scan(pair_block, jnp.zeros((), jnp.float32), occ_wide)  22.4 us
    unnamed x40, local copies, waits for them, and re-layouts  18.5 us
  transfers between devices with their start and end apart: 20, of which 10 were waited for; matrix products, arithmetic and copies ran while one was open for 9% of the time, Pallas kernels for 0%

commit v1 on v0

v1 whole, which is shorter than its diff:
```python
import functools

import jax
import jax.numpy as jnp
from jax import lax
from jax.experimental import pallas as pl
from jax.experimental.pallas import tpu as pltpu
from jax.sharding import PartitionSpec as P

MESH = pl.DeviceIdType.MESH
F32 = jnp.float32
BF16 = jnp.bfloat16
SHIFTS = (1, -1, 2, -2)


def rolled(value, shift):
    shift %= 128
    return value if shift == 0 else pltpu.roll(value, shift, value.ndim - 1)


def lanes(rows):
    return lax.broadcasted_iota(jnp.int32, (rows, 128), 1)


def stencil(plus1, minus1, plus2, minus2):
    return 8.0 * (plus1 - minus1) - (plus2 - minus2)


def split_halves(value):
    high = value.astype(BF16)
    return high, (value - high.astype(F32)).astype(BF16)


def columns_of(x):
    return range(-2, 6) if 0 <= x < 4 else range(4)


def kernel(
    sizes, scale,
    occ, vir, kf, dg,
    pot_out, cas_out,
    ext, own, cxo, cxl, cxr, cyo, cyhi, cylo, cyl, cyr,
    opk, zl, zr, hpk, hxl, hxr, hyl, hyr, czh, epk,
    nbuf, fxb, fyb, fzb, potb, dh, dl, ph, plow,
    cas, ra, dbuf, rb,
    send, recv, asend, arecv, bsend, brecv, osem,
):
    ngx, ngy, ngz = sizes
    gx, gy, gz = lax.axis_index("gx"), lax.axis_index("gy"), lax.axis_index("gz")

    def device(dx=0, dy=0, dz=0):
        return {
            "gx": lax.rem(gx + dx + ngx, ngx),
            "gy": lax.rem(gy + dy + ngy, ngy),
            "gz": lax.rem(gz + dz + ngz, ngz),
        }

    nb = ngy * ngz
    barrier = pltpu.get_barrier_semaphore()
    for k in range(1, ngx):
        pl.semaphore_signal(barrier, inc=1, device_id=device(dx=k), device_id_type=MESH)
    for k in range(1, nb):
        pl.semaphore_signal(
            barrier, inc=1, device_id=device(dy=k // ngz, dz=k % ngz), device_id_type=MESH
        )

    for c in range(16):
        x, y = divmod(c, 4)
        ext[4 + x, 4 + y, 0:16, :] = occ[pl.ds(c, 16, stride=16), :]
        ext[4 + x, 4 + y, 16:32, :] = vir[pl.ds(c, 16, stride=16), :]

    f0, f1, f2, f3 = (kf[pl.ds(16 * k, 16), :] for k in range(4))
    g = [dg[pl.ds(16 * k, 16), :] * (1.0 / 12.0) for k in range(3)]
    f3s = f3 * (1.0 / 144.0)
    for k, value in enumerate((f0, f1, f2, f3s, *g)):
        own[k] = value

    def combined(k):
        parts = [g[k] * f1]
        for other in range(3):
            beta = g[k] * g[other] * f2
            parts.append(beta + f3s if other == k else beta)
        return parts

    for k, value in enumerate(combined(0)):
        cxo[k] = value
    for k, value in enumerate(combined(1)):
        cyo[k] = value
    for k in range(4):
        cylo[k] = jnp.concatenate([cyo[k, 4 * x : 4 * x + 2, :] for x in range(4)], axis=0)
        cyhi[k] = jnp.concatenate([cyo[k, 4 * x + 2 : 4 * x + 4, :] for x in range(4)], axis=0)

    lane32 = lanes(32)

    def pack(at):
        total = None
        for c in range(16):
            part = rolled(at(c), 4 + 8 * c)
            total = part if total is None else jnp.where(lane32 // 8 == c, part, total)
        return total

    opk[0:32, :] = pack(lambda c: ext[4 + c // 4, 4 + c % 4])
    row16 = lax.broadcasted_iota(jnp.int32, (16, 128), 0)
    zrows = []
    for value in combined(2):
        turned = pltpu.roll(value, 4, 1, stride=8, stride_axis=0)
        zrows.append(
            jnp.sum(jnp.where(lanes(16) // 8 == row16, turned, 0.0), axis=0, keepdims=True)
        )
    opk[32:40, :] = jnp.concatenate(zrows + zrows, axis=0)

    pl.semaphore_wait(barrier, ngx - 1 + nb - 1)

    copies = {}

    def push(name, src, dst, target):
        k = len(copies)
        copies[name] = pltpu.make_async_remote_copy(
            src_ref=src, dst_ref=dst, send_sem=send.at[k], recv_sem=recv.at[k],
            device_id=target, device_id_type=MESH,
        )
        copies[name].start()

    push("zl", opk, zl, device(dz=1))
    push("zr", opk, zr, device(dz=-1))
    block = ext.at[4:8, 4:8]
    push("cyl", cyhi, cyl, device(dy=1))
    push("cyr", cylo, cyr, device(dy=-1))
    push("yl", block, ext.at[4:8, 0:4], device(dy=1))
    push("yr", block, ext.at[4:8, 8:12], device(dy=-1))
    push("cxl", cxo.at[:, 8:16], cxl, device(dx=1))
    push("cxr", cxo.at[:, 0:8], cxr, device(dx=-1))
    push("xl", block, ext.at[0:4, 4:8], device(dx=1))
    push("xr", block, ext.at[8:12, 4:8], device(dx=-1))

    def arrived(*names):
        for name in names:
            copies[name].wait_recv()

    arrived("zl", "zr")
    inner32 = lane32 % 8 < 4
    hpk[...] = jnp.where(inner32, zl[0:32, :], zr[0:32, :])
    czh[...] = jnp.where(lanes(8) % 8 < 4, zl[32:40, :], zr[32:40, :])
    push("hyl", hpk, hyl, device(dy=1))
    push("hyr", hpk, hyr, device(dy=-1))
    push("hxl", hpk, hxl, device(dx=1))
    push("hxr", hpk, hxr, device(dx=-1))

    arrived("yl", "yr")
    push("cll", ext.at[6:8, 2:4], ext.at[2:4, 2:4], device(dx=1))
    push("clr", ext.at[6:8, 8:10], ext.at[2:4, 8:10], device(dx=1))
    push("crl", ext.at[4:6, 2:4], ext.at[8:10, 2:4], device(dx=-1))
    push("crr", ext.at[4:6, 8:10], ext.at[8:10, 8:10], device(dx=-1))
    arrived("xl", "xr", "hyl", "hyr", "hxl", "hxr", "cyl", "cyr", "cxl", "cxr")
    arrived("cll", "clr", "crl", "crr")

    def edges(at, opack, hpack):
        high = jnp.where(inner32, opack, hpack)
        low = jnp.where(inner32, hpack, opack)
        for k, s in enumerate(SHIFTS):
            epk[at + k] = jnp.where(inner32, rolled(high, -s), rolled(low, -s))
        return high, low

    halo = hpk[...]
    high, low = edges(0, opk[0:32, :], halo)
    xpack = pack(lambda c: ext[(8 if c // 4 < 2 else 0) + c // 4, 4 + c % 4])
    edges(4, xpack, jnp.where(lane32 < 64, hxr[...], hxl[...]))
    ypack = pack(lambda c: ext[4 + c // 4, (8 if c % 4 < 2 else 0) + c % 4])
    edges(8, ypack, jnp.where(lane32 % 32 < 16, hyr[...], hyl[...]))
    epk[12] = halo
    for k, s in enumerate(SHIFTS):
        side_x, side_y = (hxr, hyr) if s > 0 else (hxl, hyl)
        inside_x = lane32 < 128 - 32 * s if s > 0 else lane32 >= -32 * s
        inside_y = lane32 % 32 < 32 - 8 * s if s > 0 else lane32 % 32 >= -8 * s
        epk[13 + k] = jnp.where(inside_x, rolled(halo, -32 * s), rolled(side_x[...], -32 * s))
        over = 32 - 8 * s if s > 0 else -32 - 8 * s
        epk[17 + k] = jnp.where(inside_y, rolled(halo, -8 * s), rolled(side_y[...], over))
        epk[21 + k] = jnp.where(inner32, rolled(low, -s), rolled(high, -s))

    lane16 = lanes(16)
    rim = (lane16 < 2) | (lane16 >= 126)

    def wide(row):
        return jnp.broadcast_to(row, (16, 128))

    def per_orbital(i, carry):
        def packed(k):
            return wide(epk[k, pl.ds(i, 1), :]) * epk[k, 16:32, :]

        def packed_slope(at):
            return stencil(*(packed(at + k) for k in range(4)))

        rims = [packed_slope(4 * k) for k in range(3)]
        zedge = (
            wide(czh[0:1, :]) * packed(12)
            + wide(czh[1:2, :]) * packed_slope(13)
            + wide(czh[2:3, :]) * packed_slope(17)
            + wide(czh[3:4, :]) * packed_slope(21)
        )

        for x in range(-4, 8):
            if 0 <= x < 4:
                ys = range(-4, 8)
            elif -2 <= x < 6:
                ys = range(-2, 6)
            else:
                ys = range(4)
            for y in ys:
                at = (4 + x, 4 + y)
                nbuf[at[0], at[1]] = wide(ext[at[0], at[1], pl.ds(i, 1), :]) * ext[at[0], at[1], 16:32, :]

        for x in range(-2, 6):
            inside = 0 <= x < 4
            line = {y: nbuf[4 + x, 4 + y] for y in (range(-4, 8) if inside else range(-2, 6))}
            for y in columns_of(x):
                n = line[y]
                sx = stencil(*(nbuf[4 + x + s, 4 + y] for s in SHIFTS))
                sy = stencil(*(line[y + s] for s in SHIFTS))
                sz = stencil(*(rolled(n, -s) for s in SHIFTS))
                c = (x % 4) * 4 + y % 4
                kind = 1 if not inside else (2 if not 0 <= y < 4 else 0)
                sz = jnp.where(rim, rolled(rims[kind], 124 - 8 * c), sz)
                if kind == 0:
                    f0, f1, f2, f3, g0, g1, g2 = (wide(own[k, c : c + 1, :]) for k in range(7))
                    aligned = g0 * sx + g1 * sy + g2 * sz
                    scalar = f1 * n + f2 * aligned
                    fxb[x + 2, y] = scalar * g0 + f3 * sx
                    fyb[x, y + 2] = scalar * g1 + f3 * sy
                    fzb[c] = scalar * g2 + f3 * sz
                    potb[c, pl.ds(pl.multiple_of(i * 16, 16), 16), :] = f0 * n + f1 * aligned
                else:
                    if kind == 1:
                        ref, row = (cxl, (x + 2) * 4 + y) if x < 0 else (cxr, (x - 4) * 4 + y)
                    else:
                        ref, row = (cyl, x * 2 + y + 2) if y < 0 else (cyr, x * 2 + y - 4)
                    c0, c1, c2, c3 = (wide(ref[k, row : row + 1, :]) for k in range(4))
                    flux = c0 * n + c1 * sx + c2 * sy + c3 * sz
                    if kind == 1:
                        fxb[x + 2, y] = flux
                    else:
                        fyb[x, y + 2] = flux

        rows = pl.ds(pl.multiple_of(i * 16, 16), 16)
        for c in range(16):
            x, y = divmod(c, 4)
            dx = stencil(*(fxb[x + 2 + s, y] for s in SHIFTS))
            dy = stencil(*(fyb[x, y + 2 + s] for s in SHIFTS))
            flux = fzb[c]
            near = []
            for s in SHIFTS:
                beyond = lane16 >= 128 - s if s > 0 else lane16 < -s
                over = (124 - s if s > 0 else 124 - s) - 8 * c
                near.append(jnp.where(beyond, rolled(zedge, over), rolled(flux, -s)))
            dz = stencil(*near)
            value = potb[c, rows, :] - (dx + dy + dz)
            potb[c, rows, :] = value
            high, low = split_halves(value)
            ph[rows, 128 * c : 128 * c + 128] = high
            plow[rows, 128 * c : 128 * c + 128] = low
            high, low = split_halves(nbuf[4 + x, 4 + y])
            dh[rows, 128 * c : 128 * c + 128] = high
            dl[rows, 128 * c : 128 * c + 128] = low
        pltpu.make_async_copy(potb.at[:, rows, :], pot_out.at[:, rows, :], osem.at[i]).start()
        return carry

    lax.fori_loop(0, 16, per_orbital, 0)

    def product(a, b):
        return lax.dot_general(a[...], b[...], (((1,), (1,)), ((), ())), preferred_element_type=F32)

    sums = (product(dh, ph) + product(dh, plow) + product(dl, ph)) * scale
    for k in range(ngx):
        cas[k] = sums[nb * k : nb * (k + 1), :]

    first = []
    for k in range(1, ngx):
        copy = pltpu.make_async_remote_copy(
            src_ref=cas.at[lax.rem(gx + k, ngx)], dst_ref=ra.at[k],
            send_sem=asend.at[k], recv_sem=arecv.at[k],
            device_id=device(dx=k), device_id_type=MESH,
        )
        copy.start()
        first.append(copy)
    for copy in first:
        copy.wait_recv()
    part = cas[gx]
    for k in range(1, ngx):
        part = part + ra[k]
    for r in range(nb):
        dbuf[r] = part[r : r + 1, :]
    second = []
    for k in range(1, nb):
        dy, dz = k // ngz, k % ngz
        there = device(dy=dy, dz=dz)
        copy = pltpu.make_async_remote_copy(
            src_ref=dbuf.at[there["gy"] * ngz + there["gz"]], dst_ref=rb.at[k],
            send_sem=bsend.at[k], recv_sem=brecv.at[k],
            device_id=there, device_id_type=MESH,
        )
        copy.start()
        second.append(copy)
    for copy in second:
        copy.wait_recv()
    row = dbuf[gy * ngz + gz]
    for k in range(1, nb):
        row = row + rb[k]
    cas_out[...] = row

    for copy in (*copies.values(), *first, *second):
        copy.wait_send()

    def drain(i, carry):
        rows = pl.ds(pl.multiple_of(i * 16, 16), 16)
        pltpu.make_async_copy(potb.at[:, rows, :], pot_out.at[:, rows, :], osem.at[i]).wait()
        return carry

    lax.fori_loop(0, 16, drain, 0)


def on_device(sizes, scale, occupied, virtual, kernel_fields, density_grad):
    ngx, ngy, ngz = sizes
    nb = ngy * ngz
    vmem = pltpu.VMEM
    dma = pltpu.SemaphoreType.DMA
    scratch = [
        vmem((12, 12, 32, 128), F32), vmem((7, 16, 128), F32),
        vmem((4, 16, 128), F32), vmem((4, 8, 128), F32), vmem((4, 8, 128), F32),
        vmem((4, 16, 128), F32), vmem((4, 8, 128), F32), vmem((4, 8, 128), F32),
        vmem((4, 8, 128), F32), vmem((4, 8, 128), F32),
        vmem((40, 128), F32), vmem((40, 128), F32), vmem((40, 128), F32),
        vmem((32, 128), F32), vmem((32, 128), F32), vmem((32, 128), F32),
        vmem((32, 128), F32), vmem((32, 128), F32), vmem((8, 128), F32),
        vmem((25, 32, 128), F32),
        vmem((12, 12, 16, 128), F32), vmem((8, 4, 16, 128), F32), vmem((4, 8, 16, 128), F32),
        vmem((16, 16, 128), F32), vmem((16, 256, 128), F32),
        vmem((256, 2048), BF16), vmem((256, 2048), BF16),
        vmem((256, 2048), BF16), vmem((256, 2048), BF16),
        vmem((ngx, nb, 256), F32), vmem((ngx, nb, 256), F32),
        vmem((nb, 1, 256), F32), vmem((nb, 1, 256), F32),
        dma((18,)), dma((18,)), dma((ngx,)), dma((ngx,)), dma((nb,)), dma((nb,)), dma((16,)),
    ]
    inner = pl.BlockSpec(memory_space=pltpu.VMEM)
    potential, row = pl.pallas_call(
        functools.partial(kernel, sizes, scale),
        out_shape=(
            jax.ShapeDtypeStruct((16, 256, 128), F32),
            jax.ShapeDtypeStruct((1, 256), F32),
        ),
        in_specs=[inner] * 4,
        out_specs=(pl.BlockSpec(memory_space=pl.ANY), inner),
        scratch_shapes=scratch,
        compiler_params=pltpu.CompilerParams(
            collective_id=0, has_side_effects=True, vmem_limit_bytes=48 * 1024 * 1024
        ),
    )(
        occupied.reshape(256, 128), virtual.reshape(256, 128),
        kernel_fields.reshape(64, 128), density_grad.reshape(48, 128),
    )
    return potential.transpose(1, 0, 2).reshape(256, 4, 4, 128), row


def solution(mesh):
    sizes = tuple(mesh.shape[axis] for axis in ("gx", "gy", "gz"))
    scale = 1.0 / (2048 * sizes[0] * sizes[1] * sizes[2])
    placed = P(None, "gx", "gy", "gz")
    return jax.shard_map(
        functools.partial(on_device, sizes, scale),
        mesh=mesh,
        in_specs=(placed,) * 4,
        out_specs=(placed, P(("gx", "gy", "gz"), None)),
        check_vma=False,
    )
```

time: 408 us -> 65.3 us (0.16); the launches traced: 402 us -> 65 us
  other arithmetic: 137 us -> 0 us
  waiting for transfers between devices: 106 us -> 0 us
  Pallas kernels: 0 us -> 57.8 us
  local copies, waits for them, and re-layouts: 62 us -> 6.53 us
  starting transfers between devices: 36.1 us -> 0 us
  blocking collectives: 30.7 us -> 0 us
  between operations: 16.9 us -> 0.65 us
  matrix products: 12 us -> 0 us
    unnamed x4 -> x0, waiting for transfers between devices: 74.5 us -> none
    add x32 -> x0, other arithmetic: 62.8 us -> none  [pair_block(): scalar * field_wide[4 + dimension] + field_wide[3] * slopes[dimension]]
    pallas_call x0 -> x1, Pallas kernels: none -> 57.8 us  [on_device(): pl.pallas_call(functools.partial(kernel, sizes, scale), out_shape=(jax.Sh...]
    mul x49 -> x0, other arithmetic: 39.2 us -> none  [the longest x16 16.4 us: pair_block(): field_wide[5] * slopes[1]]
    ppermute x18 -> x0, starting transfers between devices: 36 us -> none  [the longest x9 23.6 us: padded(): lax.ppermute(lax.slice_in_dim(block, 0, width, axis=dim), axis, backward)]
    ppermute x18 -> x0, waiting for transfers between devices: 31.6 us -> none  [the longest x9 24 us: padded(): lax.ppermute(lax.slice_in_dim(block, block.shape[dim] - width, None, axis...]
    unnamed x3 -> x0, blocking collectives: 30.7 us -> none
    dynamic_update_slice x16 -> x0, other arithmetic: 26.2 us -> none  [on_device(): lax.scan(pair_block, jnp.zeros((), jnp.float32), occ_wide)]
  transfers between devices with their start and end apart: 20 -> 0, of which waited for: 10 -> 0; matrix products, arithmetic and copies ran while one was open for 9% -> 0% of each run, Pallas kernels for 0% -> 0%
where the time goes in v1:
time: 65.3 us; the launch traced here: 65 us
  Pallas kernels  57.8 us (89%)
  local copies, waits for them, and re-layouts  6.53 us (10%)
    pallas_call x1, Pallas kernels, on_device(): pl.pallas_call(functools.partial(kernel, sizes, scale), out_shape=(jax.Sh...  57.8 us
    unnamed x10, local copies, waits for them, and re-layouts  6.53 us

profile of v1, /device:TPU:1, one launch (start us, length us, event | category | flops | bytes accessed | tf_op | source)
XLA Modules:
  0.0 65.0 jit_solution(10814937060770546144)
XLA Ops:
  0.6 0.0 copy-start
  0.6 0.9 %copy-done = f32[16,4,4,128]{3,2,1,0:T(4,128)S(1)} copy-done((f32[16,4,4,128]{3,2,1,0:T(4,128)S(1)}, f32[16,4,4,128]{3,2,1,0:T(4,128)}, u32[]{:S(2)}) %copy-start) | copy-done | bytes 131096
  1.5 0.0 copy-start.1
  1.5 0.9 %copy-done.1 = f32[16,4,4,128]{3,2,1,0:T(4,128)S(1)} copy-done((f32[16,4,4,128]{3,2,1,0:T(4,128)S(1)}, f32[16,4,4,128]{3,2,1,0:T(4,128)}, u32[]{:S(2)}) %copy-start.1) | copy-done | bytes 131096
  2.4 0.0 copy-start.2
  2.4 0.8 %copy-done.2 = f32[4,4,4,128]{3,2,1,0:T(4,128)S(1)} copy-done((f32[4,4,4,128]{3,2,1,0:T(4,128)S(1)}, f32[4,4,4,128]{3,2,1,0:T(4,128)}, u32[]{:S(2)}) %copy-start.2) | copy-done | bytes 32792
  3.2 0.0 copy-start.3
  3.2 0.7 %copy-done.3 = f32[3,4,4,128]{3,2,1,0:T(4,128)S(1)} copy-done((f32[3,4,4,128]{3,2,1,0:T(4,128)S(1)}, f32[3,4,4,128]{3,2,1,0:T(4,128)}, u32[]{:S(2)}) %copy-start.3) | copy-done | bytes 24600
  3.9 57.8 %shard_map.59 = (f32[16,256,128]{2,1,0:T(8,128)S(1)}, f32[1,256]{1,0:T(1,128)S(1)}) custom-call(f32[256,128]{1,0:T(8,128)S(1)} %bitcast.8, f32[256,128]{1,0:T(8,128)S(1)} %bitcast.9, f32[64,128]{1,0:T(8,128)S(1)} %bitcast.10, f32[48,128]{1,0:T(8,128)S(1)} %bitcast.11), custom_call_target="tpu_custom_call" | custom-call | tf_op jit(solution)/shard_map/pallas_call | solution.py:343
  61.8 2.7 %copy.6 = f32[256,4,4,128]{3,2,1,0:T(4,128)} copy(f32[256,4,4,128]{3,0,2,1:T(8,128)S(1)} %bitcast.7) | data formatting | bytes 4194304
  64.5 0.6 copy.8
Async XLA Ops:
  0.6 0.9 %copy-start = (f32[16,4,4,128]{3,2,1,0:T(4,128)S(1)}, f32[16,4,4,128]{3,2,1,0:T(4,128)}, u32[]{:S(2)}) copy-start(f32[16,4,4,128]{3,2,1,0:T(4,128)} %param.4) | copy-start | bytes 393220
  1.5 0.9 %copy-start.1 = (f32[16,4,4,128]{3,2,1,0:T(4,128)S(1)}, f32[16,4,4,128]{3,2,1,0:T(4,128)}, u32[]{:S(2)}) copy-start(f32[16,4,4,128]{3,2,1,0:T(4,128)} %param.5) | copy-start | bytes 393220
  2.4 0.8 %copy-start.2 = (f32[4,4,4,128]{3,2,1,0:T(4,128)S(1)}, f32[4,4,4,128]{3,2,1,0:T(4,128)}, u32[]{:S(2)}) copy-start(f32[4,4,4,128]{3,2,1,0:T(4,128)} %param.6) | copy-start | bytes 98308
  3.2 0.7 %copy-start.3 = (f32[3,4,4,128]{3,2,1,0:T(4,128)S(1)}, f32[3,4,4,128]{3,2,1,0:T(4,128)}, u32[]{:S(2)}) copy-start(f32[3,4,4,128]{3,2,1,0:T(4,128)} %param.7) | copy-start | bytes 73732

commit v2 on v1

v2 whole, which is shorter than its diff:
```python
import functools

import jax
import jax.numpy as jnp
from jax import lax
from jax.experimental import pallas as pl
from jax.experimental.pallas import tpu as pltpu
from jax.sharding import PartitionSpec as P

MESH = pl.DeviceIdType.MESH
F32 = jnp.float32
BF16 = jnp.bfloat16
SHIFTS = (1, -1, 2, -2)


def rolled(value, shift):
    shift %= 128
    return value if shift == 0 else pltpu.roll(value, shift, value.ndim - 1)


def lanes(rows):
    return lax.broadcasted_iota(jnp.int32, (rows, 128), 1)


def stencil(plus1, minus1, plus2, minus2):
    return 8.0 * (plus1 - minus1) - (plus2 - minus2)


def split_halves(value):
    high = value.astype(BF16)
    return high, (value - high.astype(F32)).astype(BF16)


def columns_of(x):
    return range(-2, 6) if 0 <= x < 4 else range(4)


def kernel(
    sizes, scale,
    occ_in, vir_in, kf_in, dg_in,
    pot, cas_out,
    occ, vir, kf, dg,
    ext, own, cxo, cxl, cxr, cyo, cyhi, cylo, cyl, cyr,
    opk, zl, zr, hpk, hxl, hxr, hyl, hyr, czh, epk,
    nall, nbuf, fxb, fyb, fzb, lh, ll, rh, rl, acc,
    cas, ra, dbuf, rb,
    send, recv, asend, arecv, bsend, brecv, isem, rounds,
):
    ngx, ngy, ngz = sizes
    gx, gy, gz = lax.axis_index("gx"), lax.axis_index("gy"), lax.axis_index("gz")
    nb = ngy * ngz

    def device(dx=0, dy=0, dz=0):
        return {
            "gx": lax.rem(gx + dx + ngx, ngx),
            "gy": lax.rem(gy + dy + ngy, ngy),
            "gz": lax.rem(gz + dz + ngz, ngz),
        }

    def greet(semaphore, offsets):
        for dx, dy, dz in offsets:
            pl.semaphore_signal(
                semaphore, inc=1, device_id=device(dx, dy, dz), device_id_type=MESH
            )

    nearest = [(0, 0, 1), (0, 0, -1), (0, 1, 0), (0, -1, 0), (1, 0, 0), (-1, 0, 0)]
    second_round = [(2, 0, 0), (-2, 0, 0), (0, 0, 2), (0, 0, -2)]
    second_round += [(0, dy, dz) for dy in (1, -1) for dz in (1, -1)]
    third_round = [(0, 0, 2), (0, 0, -2)]
    barrier = pltpu.get_barrier_semaphore()
    greet(barrier, nearest)

    loads = [
        pltpu.make_async_copy(src, dst, isem.at[k])
        for k, (src, dst) in enumerate(((occ_in, occ), (vir_in, vir), (kf_in, kf), (dg_in, dg)))
    ]
    for load in loads:
        load.start()
    for load in loads:
        load.wait()

    for c in range(16):
        x, y = divmod(c, 4)
        ext[4 + x, 4 + y, 0:16, :] = occ[pl.ds(c, 16, stride=16), :]
        ext[4 + x, 4 + y, 16:32, :] = vir[pl.ds(c, 16, stride=16), :]

    f0, f1, f2, f3 = (kf[pl.ds(16 * k, 16), :] for k in range(4))
    g = [dg[pl.ds(16 * k, 16), :] * (1.0 / 12.0) for k in range(3)]
    f3s = f3 * (1.0 / 144.0)
    for k, value in enumerate((f0, f1, f2, f3s, *g)):
        own[k] = value

    def combined(k):
        parts = [g[k] * f1]
        for other in range(3):
            beta = g[k] * g[other] * f2
            parts.append(beta + f3s if other == k else beta)
        return parts

    lane32 = lanes(32)

    def pack(at):
        total = None
        for c in range(16):
            part = rolled(at(c), 4 + 8 * c)
            total = part if total is None else jnp.where(lane32 // 8 == c, part, total)
        return total

    opk[0:32, :] = pack(lambda c: ext[4 + c // 4, 4 + c % 4])
    row16 = lax.broadcasted_iota(jnp.int32, (16, 128), 0)
    zrows = []
    for value in combined(2):
        turned = pltpu.roll(value, 4, 1, stride=8, stride_axis=0)
        zrows.append(
            jnp.sum(jnp.where(lanes(16) // 8 == row16, turned, 0.0), axis=0, keepdims=True)
        )
    opk[32:40, :] = jnp.concatenate(zrows + zrows, axis=0)
    for k, value in enumerate(combined(0)):
        cxo[k] = value
    for k, value in enumerate(combined(1)):
        cyo[k] = value
    for k in range(4):
        cylo[k] = jnp.concatenate([cyo[k, 4 * x : 4 * x + 2, :] for x in range(4)], axis=0)
        cyhi[k] = jnp.concatenate([cyo[k, 4 * x + 2 : 4 * x + 4, :] for x in range(4)], axis=0)

    pl.semaphore_wait(barrier, len(nearest))
    greet(rounds.at[0], nearest)

    copies = {}

    def push(name, src, dst, target):
        k = len(copies)
        copies[name] = pltpu.make_async_remote_copy(
            src_ref=src, dst_ref=dst, send_sem=send.at[k], recv_sem=recv.at[k],
            device_id=target, device_id_type=MESH,
        )
        copies[name].start()

    def arrived(*names):
        for name in names:
            copies[name].wait_recv()

    push("zl", opk, zl, device(dz=1))
    push("zr", opk, zr, device(dz=-1))
    blocks = {"v": pl.ds(16, 16), "a": pl.ds(0, 8), "b": pl.ds(8, 8), "f": pl.ds(0, 32)}
    up, down, four = pl.ds(6, 2), pl.ds(4, 2), pl.ds(4, 4)

    def push_y(kind):
        rows = blocks[kind]
        near = kind != "f"
        src, dst = (up, pl.ds(2, 2)) if near else (down, pl.ds(0, 2))
        push("yl" + kind, ext.at[four, src, rows], ext.at[four, dst, rows], device(dy=1))
        src, dst = (down, pl.ds(8, 2)) if near else (up, pl.ds(10, 2))
        push("yr" + kind, ext.at[four, src, rows], ext.at[four, dst, rows], device(dy=-1))

    def push_x(kind):
        rows = blocks[kind]
        near = kind != "f"
        src, dst = (up, pl.ds(2, 2)) if near else (down, pl.ds(0, 2))
        push("xl" + kind, ext.at[src, four, rows], ext.at[dst, four, rows], device(dx=1))
        src, dst = (down, pl.ds(8, 2)) if near else (up, pl.ds(10, 2))
        push("xr" + kind, ext.at[src, four, rows], ext.at[dst, four, rows], device(dx=-1))

    for kind in "vab":
        push_y(kind)
        push_x(kind)
    push("cyl", cyhi, cyl, device(dy=1))
    push("cyr", cylo, cyr, device(dy=-1))
    push("cxl", cxo.at[:, 8:16], cxl, device(dx=1))
    push("cxr", cxo.at[:, 0:8], cxr, device(dx=-1))

    arrived("zl", "zr")
    inner32 = lane32 % 8 < 4
    hpk[...] = jnp.where(inner32, zl[0:32, :], zr[0:32, :])
    czh[...] = jnp.where(lanes(8) % 8 < 4, zl[32:40, :], zr[32:40, :])

    def edges(at, opack, hpack):
        high = jnp.where(inner32, opack, hpack)
        low = jnp.where(inner32, hpack, opack)
        for k, s in enumerate(SHIFTS):
            epk[at + k] = jnp.where(inner32, rolled(high, -s), rolled(low, -s))
        return high, low

    halo = hpk[...]
    high, low = edges(0, opk[0:32, :], halo)
    for k, s in enumerate(SHIFTS):
        epk[21 + k] = jnp.where(inner32, rolled(low, -s), rolled(high, -s))
    epk[12] = halo

    push("hyl", hpk, hyl, device(dy=1))
    push("hyr", hpk, hyr, device(dy=-1))
    push("hxl", hpk, hxl, device(dx=1))
    push("hxr", hpk, hxr, device(dx=-1))
    push_y("f")
    push_x("f")

    pl.semaphore_wait(rounds.at[0], len(nearest))
    greet(rounds.at[1], second_round)

    lane16 = lanes(16)
    rim = (lane16 < 2) | (lane16 >= 126)

    def wide(row):
        return jnp.broadcast_to(row, (16, 128))

    def density(i, x, y):
        return wide(ext[4 + x, 4 + y, pl.ds(i, 1), :]) * ext[4 + x, 4 + y, 16:32, :]

    def packed(i, k):
        return wide(epk[k, pl.ds(i, 1), :]) * epk[k, 16:32, :]

    def packed_slope(i, at):
        return stencil(*(packed(i, at + k) for k in range(4)))

    def slope_z(n, rims, c):
        sz = stencil(*(rolled(n, -s) for s in SHIFTS))
        return jnp.where(rim, rolled(rims, 124 - 8 * c), sz)

    def corners():
        for name, src, dst, target in (
            ("cll", ext.at[up, pl.ds(2, 2)], ext.at[pl.ds(2, 2), pl.ds(2, 2)], 1),
            ("clr", ext.at[up, pl.ds(8, 2)], ext.at[pl.ds(2, 2), pl.ds(8, 2)], 1),
            ("crl", ext.at[down, pl.ds(2, 2)], ext.at[pl.ds(8, 2), pl.ds(2, 2)], -1),
            ("crr", ext.at[down, pl.ds(8, 2)], ext.at[pl.ds(8, 2), pl.ds(8, 2)], -1),
        ):
            push(name, src, dst, device(dx=target))

    arrived("ylv", "yrv", "xlv", "xrv", "yla", "yra", "xla", "xra")
    pl.semaphore_wait(rounds.at[1], len(second_round))
    greet(rounds.at[2], third_round)

    def first_pass(i, carry):
        rows = pl.ds(pl.multiple_of(i * 16, 16), 16)

        def keep(term, c, left, right):
            at = slice(128 * c, 128 * c + 128)
            lh[term, rows, at], ll[term, rows, at] = split_halves(left)
            rh[term, rows, at], rl[term, rows, at] = split_halves(right)

        rims = packed_slope(i, 0)
        for x in range(-2, 6):
            for y in columns_of(x):
                nall[i, x + 2, y + 2] = density(i, x, y)
        for x in range(4):
            line = {y: nall[i, x + 2, y + 2] for y in range(-2, 6)}
            for y in range(4):
                n = line[y]
                c = 4 * x + y
                sx = stencil(*(nall[i, x + 2 + s, y + 2] for s in SHIFTS))
                sy = stencil(*(line[y + s] for s in SHIFTS))
                sz = slope_z(n, rims, c)
                f0, f1, f2, f3, g0, g1, g2 = (wide(own[k, c : c + 1, :]) for k in range(7))
                aligned = g0 * sx + g1 * sy + g2 * sz
                scalar = f1 * n + f2 * aligned
                flux = scalar * g0 + f3 * sx
                fxb[i, x + 2, y] = flux
                keep(1, c, sx, flux)
                flux = scalar * g1 + f3 * sy
                fyb[i, x, y + 2] = flux
                keep(2, c, sy, flux)
                flux = scalar * g2 + f3 * sz
                fzb[i, c] = flux
                keep(3, c, sz, flux)
                local = f0 * n + f1 * aligned
                pot[c, rows, :] = local
                keep(0, c, n, local)
        return carry

    lax.fori_loop(0, 8, first_pass, 0)
    arrived("ylb", "yrb", "xlb", "xrb")
    corners()
    lax.fori_loop(8, 16, first_pass, 0)

    def product(a, b):
        return lax.dot_general(a, b, (((1,), (1,)), ((), ())), preferred_element_type=F32)

    acc[...] = jnp.zeros_like(acc)

    def multiply(t, carry):
        acc[...] += product(lh[t], rh[t]) + product(lh[t], rl[t]) + product(ll[t], rh[t])
        return carry

    lax.fori_loop(0, 4, multiply, 0)
    for k in range(ngx):
        cas[k] = acc[nb * k : nb * (k + 1), :] * scale

    pl.semaphore_wait(rounds.at[2], len(third_round))
    first = []
    for k in range(1, ngx):
        copy = pltpu.make_async_remote_copy(
            src_ref=cas.at[lax.rem(gx + k, ngx)], dst_ref=ra.at[k],
            send_sem=asend.at[k], recv_sem=arecv.at[k],
            device_id=device(dx=k), device_id_type=MESH,
        )
        copy.start()
        first.append(copy)
    second = []
    for k in range(1, nb):
        there = device(dy=k // ngz, dz=k % ngz)
        second.append(
            pltpu.make_async_remote_copy(
                src_ref=dbuf.at[there["gy"] * ngz + there["gz"]], dst_ref=rb.at[k],
                send_sem=bsend.at[k], recv_sem=brecv.at[k],
                device_id=there, device_id_type=MESH,
            )
        )

    def reduce_first():
        for copy in first:
            copy.wait_recv()
        part = cas[gx]
        for k in range(1, ngx):
            part = part + ra[k]
        for r in range(nb):
            dbuf[r] = part[r : r + 1, :]
        for copy in second:
            copy.start()

    arrived("xlf", "xrf", "ylf", "yrf", "hyl", "hyr", "hxl", "hxr", "cyl", "cyr", "cxl", "cxr")
    arrived("cll", "clr", "crl", "crr")
    xpack = pack(lambda c: ext[(8 if c // 4 < 2 else 0) + c // 4, 4 + c % 4])
    edges(4, xpack, jnp.where(lane32 < 64, hxr[...], hxl[...]))
    ypack = pack(lambda c: ext[4 + c // 4, (8 if c % 4 < 2 else 0) + c % 4])
    edges(8, ypack, jnp.where(lane32 % 32 < 16, hyr[...], hyl[...]))
    halo = hpk[...]
    for k, s in enumerate(SHIFTS):
        side_x, side_y = (hxr, hyr) if s > 0 else (hxl, hyl)
        inside_x = lane32 < 128 - 32 * s if s > 0 else lane32 >= -32 * s
        inside_y = lane32 % 32 < 32 - 8 * s if s > 0 else lane32 % 32 >= -8 * s
        epk[13 + k] = jnp.where(inside_x, rolled(halo, -32 * s), rolled(side_x[...], -32 * s))
        over = 32 - 8 * s if s > 0 else -32 - 8 * s
        epk[17 + k] = jnp.where(inside_y, rolled(halo, -8 * s), rolled(side_y[...], over))

    def second_pass(i, carry):
        rows = pl.ds(pl.multiple_of(i * 16, 16), 16)

        def at(x, y):
            if (0 <= x < 4 and -2 <= y < 6) or (0 <= y < 4 and -2 <= x < 6):
                return nall[i, x + 2, y + 2]
            return nbuf[x + 4, y + 4]

        rims = {4: packed_slope(i, 4), 8: packed_slope(i, 8)}
        zedge = (
            wide(czh[0:1, :]) * packed(i, 12)
            + wide(czh[1:2, :]) * packed_slope(i, 13)
            + wide(czh[2:3, :]) * packed_slope(i, 17)
            + wide(czh[3:4, :]) * packed_slope(i, 21)
        )
        for x in (-4, -3, -2, -1, 0, 1, 2, 3, 4, 5, 6, 7):
            if 0 <= x < 4:
                ys = (-4, -3, 6, 7)
            elif -2 <= x < 6:
                ys = (-2, -1, 4, 5)
            else:
                ys = (0, 1, 2, 3)
            for y in ys:
                nbuf[4 + x, 4 + y] = density(i, x, y)

        def halo_flux(x, y, refs, row, at_pack):
            n = at(x, y)
            sx = stencil(*(at(x + s, y) for s in SHIFTS))
            sy = stencil(*(at(x, y + s) for s in SHIFTS))
            sz = slope_z(n, rims[at_pack], (x % 4) * 4 + y % 4)
            c0, c1, c2, c3 = (wide(refs[k, row : row + 1, :]) for k in range(4))
            return c0 * n + c1 * sx + c2 * sy + c3 * sz

        for x in (-2, -1, 4, 5):
            for y in range(4):
                refs, row = (cxl, (x + 2) * 4 + y) if x < 0 else (cxr, (x - 4) * 4 + y)
                fxb[i, x + 2, y] = halo_flux(x, y, refs, row, 4)
        for x in range(4):
            for y in (-2, -1, 4, 5):
                refs, row = (cyl, x * 2 + y + 2) if y < 0 else (cyr, x * 2 + y - 4)
                fyb[i, x, y + 2] = halo_flux(x, y, refs, row, 8)

        for c in range(16):
            x, y = divmod(c, 4)
            dx = stencil(*(fxb[i, x + 2 + s, y] for s in SHIFTS))
            dy = stencil(*(fyb[i, x, y + 2 + s] for s in SHIFTS))
            flux = fzb[i, c]
            near = []
            for s in SHIFTS:
                beyond = lane16 >= 128 - s if s > 0 else lane16 < -s
                near.append(jnp.where(beyond, rolled(zedge, 124 - s - 8 * c), rolled(flux, -s)))
            dz = stencil(*near)
            pot[c, rows, :] = pot[c, rows, :] - (dx + dy + dz)
        return carry

    lax.fori_loop(0, 8, second_pass, 0)
    reduce_first()
    lax.fori_loop(8, 16, second_pass, 0)

    for copy in second:
        copy.wait_recv()
    row = dbuf[gy * ngz + gz]
    for k in range(1, nb):
        row = row + rb[k]
    cas_out[...] = row
    for copy in (*copies.values(), *first, *second):
        copy.wait_send()


def on_device(sizes, scale, occupied, virtual, kernel_fields, density_grad):
    ngx, ngy, ngz = sizes
    nb = ngy * ngz
    vmem = pltpu.VMEM
    dma = pltpu.SemaphoreType.DMA
    scratch = [
        vmem((256, 128), F32), vmem((256, 128), F32), vmem((64, 128), F32), vmem((48, 128), F32),
        vmem((12, 12, 32, 128), F32), vmem((7, 16, 128), F32),
        vmem((4, 16, 128), F32), vmem((4, 8, 128), F32), vmem((4, 8, 128), F32),
        vmem((4, 16, 128), F32), vmem((4, 8, 128), F32), vmem((4, 8, 128), F32),
        vmem((4, 8, 128), F32), vmem((4, 8, 128), F32),
        vmem((40, 128), F32), vmem((40, 128), F32), vmem((40, 128), F32),
        vmem((32, 128), F32), vmem((32, 128), F32), vmem((32, 128), F32),
        vmem((32, 128), F32), vmem((32, 128), F32), vmem((8, 128), F32),
        vmem((25, 32, 128), F32),
        vmem((16, 8, 8, 16, 128), F32), vmem((12, 12, 16, 128), F32),
        vmem((16, 8, 4, 16, 128), F32), vmem((16, 4, 8, 16, 128), F32), vmem((16, 16, 16, 128), F32),
        vmem((4, 256, 2048), BF16), vmem((4, 256, 2048), BF16),
        vmem((4, 256, 2048), BF16), vmem((4, 256, 2048), BF16), vmem((256, 256), F32),
        vmem((ngx, nb, 256), F32), vmem((ngx, nb, 256), F32),
        vmem((nb, 1, 256), F32), vmem((nb, 1, 256), F32),
        dma((32,)), dma((32,)), dma((ngx,)), dma((ngx,)), dma((nb,)), dma((nb,)), dma((4,)),
        pltpu.SemaphoreType.REGULAR((3,)),
    ]
    inner = pl.BlockSpec(memory_space=pltpu.VMEM)
    potential, row = pl.pallas_call(
        functools.partial(kernel, sizes, scale),
        out_shape=(
            jax.ShapeDtypeStruct((16, 256, 128), F32),
            jax.ShapeDtypeStruct((1, 256), F32),
        ),
        in_specs=[pl.BlockSpec(memory_space=pltpu.HBM)] * 4,
        out_specs=(inner, inner),
        scratch_shapes=scratch,
        compiler_params=pltpu.CompilerParams(
            collective_id=0, has_side_effects=True, vmem_limit_bytes=44 * 1024 * 1024
        ),
    )(
        occupied.reshape(256, 128), virtual.reshape(256, 128),
        kernel_fields.reshape(64, 128), density_grad.reshape(48, 128),
    )
    return potential.transpose(1, 0, 2).reshape(256, 4, 4, 128), row


def solution(mesh):
    sizes = tuple(mesh.shape[axis] for axis in ("gx", "gy", "gz"))
    scale = 1.0 / (2048 * sizes[0] * sizes[1] * sizes[2])
    placed = P(None, "gx", "gy", "gz")
    return jax.shard_map(
        functools.partial(on_device, sizes, scale),
        mesh=mesh,
        in_specs=(placed,) * 4,
        out_specs=(placed, P(("gx", "gy", "gz"), None)),
        check_vma=False,
    )
```

time: 65.3 us -> 51.2 us (0.78)
  Pallas kernels: 57.8 us -> 43.4 us
    pallas_call x1, Pallas kernels: 57.8 us -> 43.4 us  [on_device(): pl.pallas_call(functools.partial(kernel, sizes, scale), out_shape=(jax.Sh...]
where the time goes in v2:
time: 51.2 us; the launch traced here: 50.6 us
  Pallas kernels  43.4 us (85%)
  local copies, waits for them, and re-layouts  6.53 us (13%)
  between operations  0.65 us (1%)
    pallas_call x1, Pallas kernels, on_device(): pl.pallas_call(functools.partial(kernel, sizes, scale), out_shape=(jax.Sh...  43.4 us
    unnamed x10, local copies, waits for them, and re-layouts  6.53 us

profile of v2, /device:TPU:1, one launch (start us, length us, event | category | flops | bytes accessed | tf_op | source)
XLA Modules:
  0.0 50.6 jit_solution(17718367156924418884)
XLA Ops:
  0.6 0.0 copy-start
  0.6 0.9 %copy-done = f32[16,4,4,128]{3,2,1,0:T(4,128)S(1)} copy-done((f32[16,4,4,128]{3,2,1,0:T(4,128)S(1)}, f32[16,4,4,128]{3,2,1,0:T(4,128)}, u32[]{:S(2)}) %copy-start) | copy-done | bytes 131096
  1.5 0.0 copy-start.1
  1.5 0.9 %copy-done.1 = f32[16,4,4,128]{3,2,1,0:T(4,128)S(1)} copy-done((f32[16,4,4,128]{3,2,1,0:T(4,128)S(1)}, f32[16,4,4,128]{3,2,1,0:T(4,128)}, u32[]{:S(2)}) %copy-start.1) | copy-done | bytes 131096
  2.4 0.0 copy-start.2
  2.4 0.8 %copy-done.2 = f32[4,4,4,128]{3,2,1,0:T(4,128)S(1)} copy-done((f32[4,4,4,128]{3,2,1,0:T(4,128)S(1)}, f32[4,4,4,128]{3,2,1,0:T(4,128)}, u32[]{:S(2)}) %copy-start.2) | copy-done | bytes 32792
  3.2 0.0 copy-start.3
  3.2 0.7 %copy-done.3 = f32[3,4,4,128]{3,2,1,0:T(4,128)S(1)} copy-done((f32[3,4,4,128]{3,2,1,0:T(4,128)S(1)}, f32[3,4,4,128]{3,2,1,0:T(4,128)}, u32[]{:S(2)}) %copy-start.3) | copy-done | bytes 24600
  3.9 43.4 %shard_map.59 = (f32[16,256,128]{2,1,0:T(8,128)S(1)}, f32[1,256]{1,0:T(1,128)S(1)}) custom-call(f32[256,128]{1,0:T(8,128)S(1)} %bitcast.8, f32[256,128]{1,0:T(8,128)S(1)} %bitcast.9, f32[64,128]{1,0:T(8,128)S(1)} %bitcast.10, f32[48,128]{1,0:T(8,128)S(1)} %bitcast.11), custom_call_target="tpu_custom_call" | custom-call | tf_op jit(solution)/shard_map/pallas_call | solution.py:428
  47.3 2.7 %copy.6 = f32[256,4,4,128]{3,2,1,0:T(4,128)} copy(f32[256,4,4,128]{3,0,2,1:T(8,128)S(1)} %bitcast.7) | data formatting | bytes 4194304
  50.0 0.6 %copy.8 = f32[1,256]{1,0:T(1,128)} copy(f32[1,256]{1,0:T(1,128)S(1)} %get-tuple-element.11) | data formatting | bytes 2048
Async XLA Ops:
  0.6 0.9 %copy-start = (f32[16,4,4,128]{3,2,1,0:T(4,128)S(1)}, f32[16,4,4,128]{3,2,1,0:T(4,128)}, u32[]{:S(2)}) copy-start(f32[16,4,4,128]{3,2,1,0:T(4,128)} %param.4) | copy-start | bytes 393220
  1.5 0.9 %copy-start.1 = (f32[16,4,4,128]{3,2,1,0:T(4,128)S(1)}, f32[16,4,4,128]{3,2,1,0:T(4,128)}, u32[]{:S(2)}) copy-start(f32[16,4,4,128]{3,2,1,0:T(4,128)} %param.5) | copy-start | bytes 393220
  2.4 0.8 %copy-start.2 = (f32[4,4,4,128]{3,2,1,0:T(4,128)S(1)}, f32[4,4,4,128]{3,2,1,0:T(4,128)}, u32[]{:S(2)}) copy-start(f32[4,4,4,128]{3,2,1,0:T(4,128)} %param.6) | copy-start | bytes 98308
  3.2 0.7 %copy-start.3 = (f32[3,4,4,128]{3,2,1,0:T(4,128)S(1)}, f32[3,4,4,128]{3,2,1,0:T(4,128)}, u32[]{:S(2)}) copy-start(f32[3,4,4,128]{3,2,1,0:T(4,128)} %param.7) | copy-start | bytes 73732

commit v3 on v2

--- a/solution.py
+++ b/solution.py
@@ -37,14 +37,13 @@
 
 def kernel(
     sizes, scale,
-    occ_in, vir_in, kf_in, dg_in,
+    everything,
     pot, cas_out,
-    occ, vir, kf, dg,
     ext, own, cxo, cxl, cxr, cyo, cyhi, cylo, cyl, cyr,
     opk, zl, zr, hpk, hxl, hxr, hyl, hyr, czh, epk,
-    nall, nbuf, fxb, fyb, fzb, lh, ll, rh, rl, acc,
+    nall, nbuf, fxb, fyb, fzb, local_pot, lh, ll, rh, rl, acc,
     cas, ra, dbuf, rb,
-    send, recv, asend, arecv, bsend, brecv, isem, rounds,
+    send, recv, asend, arecv, bsend, brecv, rounds,
 ):
     ngx, ngy, ngz = sizes
     gx, gy, gz = lax.axis_index("gx"), lax.axis_index("gy"), lax.axis_index("gz")
@@ -70,22 +69,13 @@
     barrier = pltpu.get_barrier_semaphore()
     greet(barrier, nearest)
 
-    loads = [
-        pltpu.make_async_copy(src, dst, isem.at[k])
-        for k, (src, dst) in enumerate(((occ_in, occ), (vir_in, vir), (kf_in, kf), (dg_in, dg)))
-    ]
-    for load in loads:
-        load.start()
-    for load in loads:
-        load.wait()
-
     for c in range(16):
         x, y = divmod(c, 4)
-        ext[4 + x, 4 + y, 0:16, :] = occ[pl.ds(c, 16, stride=16), :]
-        ext[4 + x, 4 + y, 16:32, :] = vir[pl.ds(c, 16, stride=16), :]
-
-    f0, f1, f2, f3 = (kf[pl.ds(16 * k, 16), :] for k in range(4))
-    g = [dg[pl.ds(16 * k, 16), :] * (1.0 / 12.0) for k in range(3)]
+        ext[4 + x, 4 + y, 0:16, :] = everything[pl.ds(c, 16, stride=16), :]
+        ext[4 + x, 4 + y, 16:32, :] = everything[pl.ds(256 + c, 16, stride=16), :]
+
+    f0, f1, f2, f3 = (everything[pl.ds(512 + 16 * k, 16), :] for k in range(4))
+    g = [everything[pl.ds(576 + 16 * k, 16), :] * (1.0 / 12.0) for k in range(3)]
     f3s = f3 * (1.0 / 144.0)
     for k, value in enumerate((f0, f1, f2, f3s, *g)):
         own[k] = value
@@ -194,9 +184,6 @@
     push_y("f")
     push_x("f")
 
-    pl.semaphore_wait(rounds.at[0], len(nearest))
-    greet(rounds.at[1], second_round)
-
     lane16 = lanes(16)
     rim = (lane16 < 2) | (lane16 >= 126)
 
@@ -226,16 +213,15 @@
             push(name, src, dst, device(dx=target))
 
     arrived("ylv", "yrv", "xlv", "xrv", "yla", "yra", "xla", "xra")
-    pl.semaphore_wait(rounds.at[1], len(second_round))
-    greet(rounds.at[2], third_round)
+    pl.semaphore_wait(rounds.at[0], len(nearest))
+    greet(rounds.at[1], second_round)
 
     def first_pass(i, carry):
         rows = pl.ds(pl.multiple_of(i * 16, 16), 16)
 
         def keep(term, c, left, right):
-            at = slice(128 * c, 128 * c + 128)
-            lh[term, rows, at], ll[term, rows, at] = split_halves(left)
-            rh[term, rows, at], rl[term, rows, at] = split_halves(right)
+            lh[term, c, rows, :], ll[term, c, rows, :] = split_halves(left)
+            rh[term, c, rows, :], rl[term, c, rows, :] = split_halves(right)
 
         rims = packed_slope(i, 0)
         for x in range(-2, 6):
@@ -262,13 +248,15 @@
                 fzb[i, c] = flux
                 keep(3, c, sz, flux)
                 local = f0 * n + f1 * aligned
-                pot[c, rows, :] = local
+                local_pot[i, c] = local
                 keep(0, c, n, local)
         return carry
 
     lax.fori_loop(0, 8, first_pass, 0)
     arrived("ylb", "yrb", "xlb", "xrb")
     corners()
+    pl.semaphore_wait(rounds.at[1], len(second_round))
+    greet(rounds.at[2], third_round)
     lax.fori_loop(8, 16, first_pass, 0)
 
     def product(a, b):
@@ -277,7 +265,10 @@
     acc[...] = jnp.zeros_like(acc)
 
     def multiply(t, carry):
-        acc[...] += product(lh[t], rh[t]) + product(lh[t], rl[t]) + product(ll[t], rh[t])
+        a, b, c, d = (
+            jnp.concatenate([ref[t, k] for k in range(16)], axis=1) for ref in (lh, ll, rh, rl)
+        )
+        acc[...] += product(a, c) + product(a, d) + product(b, c)
         return carry
 
     lax.fori_loop(0, 4, multiply, 0)
@@ -332,8 +323,6 @@
         epk[17 + k] = jnp.where(inside_y, rolled(halo, -8 * s), rolled(side_y[...], over))
 
     def second_pass(i, carry):
-        rows = pl.ds(pl.multiple_of(i * 16, 16), 16)
-
         def at(x, y):
             if (0 <= x < 4 and -2 <= y < 6) or (0 <= y < 4 and -2 <= x < 6):
                 return nall[i, x + 2, y + 2]
@@ -383,12 +372,12 @@
                 beyond = lane16 >= 128 - s if s > 0 else lane16 < -s
                 near.append(jnp.where(beyond, rolled(zedge, 124 - s - 8 * c), rolled(flux, -s)))
             dz = stencil(*near)
-            pot[c, rows, :] = pot[c, rows, :] - (dx + dy + dz)
+            pot[pl.ds(i * 256 + c, 16, stride=16), :] = local_pot[i, c] - (dx + dy + dz)
         return carry
 
-    lax.fori_loop(0, 8, second_pass, 0)
+    lax.fori_loop(0, 6, second_pass, 0)
     reduce_first()
-    lax.fori_loop(8, 16, second_pass, 0)
+    lax.fori_loop(6, 16, second_pass, 0)
 
     for copy in second:
         copy.wait_recv()
@@ -406,7 +395,6 @@
     vmem = pltpu.VMEM
     dma = pltpu.SemaphoreType.DMA
     scratch = [
-        vmem((256, 128), F32), vmem((256, 128), F32), vmem((64, 128), F32), vmem((48, 128), F32),
         vmem((12, 12, 32, 128), F32), vmem((7, 16, 128), F32),
         vmem((4, 16, 128), F32), vmem((4, 8, 128), F32), vmem((4, 8, 128), F32),
         vmem((4, 16, 128), F32), vmem((4, 8, 128), F32), vmem((4, 8, 128), F32),
@@ -417,31 +405,29 @@
         vmem((25, 32, 128), F32),
         vmem((16, 8, 8, 16, 128), F32), vmem((12, 12, 16, 128), F32),
         vmem((16, 8, 4, 16, 128), F32), vmem((16, 4, 8, 16, 128), F32), vmem((16, 16, 16, 128), F32),
-        vmem((4, 256, 2048), BF16), vmem((4, 256, 2048), BF16),
-        vmem((4, 256, 2048), BF16), vmem((4, 256, 2048), BF16), vmem((256, 256), F32),
+        vmem((16, 16, 16, 128), F32),
+        vmem((4, 16, 256, 128), BF16), vmem((4, 16, 256, 128), BF16),
+        vmem((4, 16, 256, 128), BF16), vmem((4, 16, 256, 128), BF16), vmem((256, 256), F32),
         vmem((ngx, nb, 256), F32), vmem((ngx, nb, 256), F32),
         vmem((nb, 1, 256), F32), vmem((nb, 1, 256), F32),
-        dma((32,)), dma((32,)), dma((ngx,)), dma((ngx,)), dma((nb,)), dma((nb,)), dma((4,)),
+        dma((32,)), dma((32,)), dma((ngx,)), dma((ngx,)), dma((nb,)), dma((nb,)),
         pltpu.SemaphoreType.REGULAR((3,)),
     ]
     inner = pl.BlockSpec(memory_space=pltpu.VMEM)
     potential, row = pl.pallas_call(
         functools.partial(kernel, sizes, scale),
         out_shape=(
-            jax.ShapeDtypeStruct((16, 256, 128), F32),
+            jax.ShapeDtypeStruct((4096, 128), F32),
             jax.ShapeDtypeStruct((1, 256), F32),
         ),
-        in_specs=[pl.BlockSpec(memory_space=pltpu.HBM)] * 4,
+        in_specs=[inner],
         out_specs=(inner, inner),
         scratch_shapes=scratch,
         compiler_params=pltpu.CompilerParams(
             collective_id=0, has_side_effects=True, vmem_limit_bytes=44 * 1024 * 1024
         ),
-    )(
-        occupied.reshape(256, 128), virtual.reshape(256, 128),
-        kernel_fields.reshape(64, 128), density_grad.reshape(48, 128),
-    )
-    return potential.transpose(1, 0, 2).reshape(256, 4, 4, 128), row
+    )(jnp.concatenate([occupied, virtual, kernel_fields, density_grad], axis=0).reshape(624, 128))
+    return potential.reshape(256, 4, 4, 128), row
 
 
 def solution(mesh):

time: 51.2 us -> 47.4 us (0.926); the launches traced: 50.6 us -> 47.3 us
  local copies, waits for them, and re-layouts: 6.53 us -> 1.88 us
  other arithmetic: 0 us -> 1.08 us
    unnamed x10 -> x2, local copies, waits for them, and re-layouts: 6.53 us -> 1.88 us
    concatenate x0 -> x1, other arithmetic: none -> 1.08 us  [on_device(): jnp.concatenate([occupied, virtual, kernel_fields, density_grad], axis=0)]
where the time goes in v3:
time: 47.4 us; the launch traced here: 47.3 us
  Pallas kernels  43.7 us (92%)
  local copies, waits for them, and re-layouts  1.88 us (4%)
  other arithmetic  1.08 us (2%)
  between operations  0.64 us (1%)
    pallas_call x1, Pallas kernels, on_device(): pl.pallas_call(functools.partial(kernel, sizes, scale), out_shape=(jax.Sh...  43.7 us
    unnamed x2, local copies, waits for them, and re-layouts  1.88 us
    concatenate x1, other arithmetic, on_device(): jnp.concatenate([occupied, virtual, kernel_fields, density_grad], axis=0)  1.08 us

profile of v3, /device:TPU:1, one launch (start us, length us, event | category | flops | bytes accessed | tf_op | source)
XLA Modules:
  0.0 47.3 jit_solution(5717734976579576147)
XLA Ops:
  0.6 1.1 %pad_maximum_fusion = f32[39,4,4,128]{3,2,1,0:T(4,128)S(1)} fusion(f32[3,4,4,128]{3,2,1,0:T(4,128)} %param.7, f32[4,4,4,128]{3,2,1,0:T(4,128)} %param.6, f32[16,4,4,128]{3,2,1,0:T(4,128)} %param.5, f32[16,4,4,128]{3,2,1,0:T(4,128)} %param.4), kind=kLoop, calls=%fused_computation | loop fusion | flops 239616 | bytes 638976 | tf_op jit(solution)/shard_map/concatenate | solution.py:429
  1.7 43.7 %shard_map.59 = (f32[4096,128]{1,0:T(8,128)S(1)}, f32[1,256]{1,0:T(1,128)S(1)}) custom-call(f32[624,128]{1,0:T(8,128)S(1)} %bitcast.3), custom_call_target="tpu_custom_call" | custom-call | tf_op jit(solution)/shard_map/pallas_call | solution.py:417
  45.5 1.3 %copy.8 = f32[256,4,4,128]{3,2,1,0:T(4,128)} copy(f32[256,4,4,128]{3,2,1,0:T(4,128)S(1)} %bitcast.2) | data formatting | bytes 4194304
  46.8 0.6 %copy.9 = f32[1,256]{1,0:T(1,128)} copy(f32[1,256]{1,0:T(1,128)S(1)} %get-tuple-element.9) | data formatting | bytes 2048

commit v4 on v3

--- a/solution.py
+++ b/solution.py
@@ -41,7 +41,7 @@
     pot, cas_out,
     ext, own, cxo, cxl, cxr, cyo, cyhi, cylo, cyl, cyr,
     opk, zl, zr, hpk, hxl, hxr, hyl, hyr, czh, epk,
-    nall, nbuf, fxb, fyb, fzb, local_pot, lh, ll, rh, rl, acc,
+    nall, nbuf, sxb, szb, fzp, shifted, halo_coef, fxb, fyb, fzb, local_pot, lf, rf,
     cas, ra, dbuf, rb,
     send, recv, asend, arecv, bsend, brecv, rounds,
 ):
@@ -78,7 +78,8 @@
     g = [everything[pl.ds(576 + 16 * k, 16), :] * (1.0 / 12.0) for k in range(3)]
     f3s = f3 * (1.0 / 144.0)
     for k, value in enumerate((f0, f1, f2, f3s, *g)):
-        own[k] = value
+        for c in range(16):
+            own[k, c] = jnp.broadcast_to(value[c : c + 1, :], (8, 128))
 
     def combined(k):
         parts = [g[k] * f1]
@@ -132,7 +133,7 @@
 
     push("zl", opk, zl, device(dz=1))
     push("zr", opk, zr, device(dz=-1))
-    blocks = {"v": pl.ds(16, 16), "a": pl.ds(0, 8), "b": pl.ds(8, 8), "f": pl.ds(0, 32)}
+    blocks = {"v": pl.ds(16, 16), "a": pl.ds(0, 4), "b": pl.ds(4, 4), "c": pl.ds(8, 8), "f": pl.ds(0, 32)}
     up, down, four = pl.ds(6, 2), pl.ds(4, 2), pl.ds(4, 4)
 
     def push_y(kind):
@@ -151,7 +152,7 @@
         src, dst = (down, pl.ds(8, 2)) if near else (up, pl.ds(10, 2))
         push("xr" + kind, ext.at[src, four, rows], ext.at[dst, four, rows], device(dx=-1))
 
-    for kind in "vab":
+    for kind in "vabc":
         push_y(kind)
         push_x(kind)
     push("cyl", cyhi, cyl, device(dy=1))
@@ -159,6 +160,44 @@
     push("cxl", cxo.at[:, 8:16], cxl, device(dx=1))
     push("cxr", cxo.at[:, 0:8], cxr, device(dx=-1))
 
+    lane16 = lanes(16)
+    rim = (lane16 < 2) | (lane16 >= 126)
+    rim32 = (lane32 < 2) | (lane32 >= 126)
+
+    def wide(row):
+        return jnp.broadcast_to(row, (16, 128))
+
+    def twice(value):
+        return jnp.concatenate([value, value], axis=0)
+
+    def rows_of(i):
+        return pl.ds(pl.multiple_of(i * 16, 16), 16)
+
+    def density(i, x, y):
+        return wide(ext[4 + x, 4 + y, pl.ds(i, 1), :]) * ext[4 + x, 4 + y, 16:32, :]
+
+    def packed(i, k):
+        return wide(epk[k, pl.ds(i, 1), :]) * epk[k, 16:32, :]
+
+    def packed_slope(i, at):
+        return stencil(*(packed(i, at + k) for k in range(4)))
+
+    def slope_z(n, rims, c):
+        sz = stencil(*(rolled(n, -s) for s in SHIFTS))
+        return jnp.where(rim, rolled(rims, 124 - 8 * c), sz)
+
+    def own_columns(i, carry):
+        rows = rows_of(i)
+        for c in range(16):
+            x, y = divmod(c, 4)
+            n = density(i, x, y)
+            nall[i, x + 2, y + 2] = n
+            szb[i, c] = stencil(*(rolled(n, -s) for s in SHIFTS))
+            lf[0, c, 0, rows, :], lf[0, c, 1, rows, :] = split_halves(n)
+        return carry
+
+    lax.fori_loop(0, 16, own_columns, 0)
+
     arrived("zl", "zr")
     inner32 = lane32 % 8 < 4
     hpk[...] = jnp.where(inner32, zl[0:32, :], zr[0:32, :])
@@ -183,25 +222,6 @@
     push("hxr", hpk, hxr, device(dx=-1))
     push_y("f")
     push_x("f")
-
-    lane16 = lanes(16)
-    rim = (lane16 < 2) | (lane16 >= 126)
-
-    def wide(row):
-        return jnp.broadcast_to(row, (16, 128))
-
-    def density(i, x, y):
-        return wide(ext[4 + x, 4 + y, pl.ds(i, 1), :]) * ext[4 + x, 4 + y, 16:32, :]
-
-    def packed(i, k):
-        return wide(epk[k, pl.ds(i, 1), :]) * epk[k, 16:32, :]
-
-    def packed_slope(i, at):
-        return stencil(*(packed(i, at + k) for k in range(4)))
-
-    def slope_z(n, rims, c):
-        sz = stencil(*(rolled(n, -s) for s in SHIFTS))
-        return jnp.where(rim, rolled(rims, 124 - 8 * c), sz)
 
     def corners():
         for name, src, dst, target in (
@@ -212,48 +232,82 @@
         ):
             push(name, src, dst, device(dx=target))
 
-    arrived("ylv", "yrv", "xlv", "xrv", "yla", "yra", "xla", "xra")
+    def coefficients(c, which):
+        return (twice(own[k, c]) for k in which)
+
+    def slopes_xz(i, carry):
+        rows = rows_of(i)
+        rims = packed_slope(i, 0)
+        for y in range(4):
+            line = {}
+            for x in range(-2, 6):
+                if 0 <= x < 4:
+                    line[x] = nall[i, x + 2, y + 2]
+                else:
+                    line[x] = density(i, x, y)
+                    nall[i, x + 2, y + 2] = line[x]
+            for x in range(4):
+                c = 4 * x + y
+                sx = stencil(*(line[x + s] for s in SHIFTS))
+                sz = jnp.where(rim, rolled(rims, 124 - 8 * c), szb[i, c])
+                g0, g2 = coefficients(c, (4, 6))
+                sxb[i, c] = sx
+                szb[i, c] = sz
+                local_pot[i, c] = g0 * sx + g2 * sz
+                for term, value in ((1, sx), (3, sz)):
+                    lf[term, c, 0, rows, :], lf[term, c, 1, rows, :] = split_halves(value)
+        return carry
+
+    arrived("xlv", "xrv", "xla", "xra", "xlb", "xrb", "xlc", "xrc")
+    lax.fori_loop(0, 16, slopes_xz, 0)
     pl.semaphore_wait(rounds.at[0], len(nearest))
     greet(rounds.at[1], second_round)
+    arrived("ylv", "yrv", "yla", "yra")
 
     def first_pass(i, carry):
-        rows = pl.ds(pl.multiple_of(i * 16, 16), 16)
-
-        def keep(term, c, left, right):
-            lh[term, c, rows, :], ll[term, c, rows, :] = split_halves(left)
-            rh[term, c, rows, :], rl[term, c, rows, :] = split_halves(right)
-
-        rims = packed_slope(i, 0)
-        for x in range(-2, 6):
-            for y in columns_of(x):
-                nall[i, x + 2, y + 2] = density(i, x, y)
+        rows = rows_of(i)
+
+        def keep(term, c, right):
+            rf[term, c, 0, rows, :], rf[term, c, 1, rows, :] = split_halves(right)
+
+        ends = None
         for x in range(4):
-            line = {y: nall[i, x + 2, y + 2] for y in range(-2, 6)}
+            line = {}
+            for y in range(-2, 6):
+                if 0 <= y < 4:
+                    line[y] = nall[i, x + 2, y + 2]
+                else:
+                    line[y] = density(i, x, y)
+                    nall[i, x + 2, y + 2] = line[y]
             for y in range(4):
                 n = line[y]
                 c = 4 * x + y
-                sx = stencil(*(nall[i, x + 2 + s, y + 2] for s in SHIFTS))
                 sy = stencil(*(line[y + s] for s in SHIFTS))
-                sz = slope_z(n, rims, c)
-                f0, f1, f2, f3, g0, g1, g2 = (wide(own[k, c : c + 1, :]) for k in range(7))
-                aligned = g0 * sx + g1 * sy + g2 * sz
+                lf[2, c, 0, rows, :], lf[2, c, 1, rows, :] = split_halves(sy)
+                f0, f1, f2, f3, g0, g1, g2 = coefficients(c, range(7))
+                aligned = local_pot[i, c] + g1 * sy
                 scalar = f1 * n + f2 * aligned
-                flux = scalar * g0 + f3 * sx
+                flux = scalar * g0 + f3 * sxb[i, c]
                 fxb[i, x + 2, y] = flux
-                keep(1, c, sx, flux)
+                keep(1, c, flux)
                 flux = scalar * g1 + f3 * sy
                 fyb[i, x, y + 2] = flux
-                keep(2, c, sy, flux)
-                flux = scalar * g2 + f3 * sz
+                keep(2, c, flux)
+                flux = scalar * g2 + f3 * szb[i, c]
                 fzb[i, c] = flux
-                keep(3, c, sz, flux)
+                keep(3, c, flux)
+                part = rolled(flux, 4 + 8 * c)
+                ends = part if ends is None else jnp.where(lane16 // 8 == c, part, ends)
                 local = f0 * n + f1 * aligned
                 local_pot[i, c] = local
-                keep(0, c, n, local)
+                keep(0, c, local)
+        fzp[i] = ends
         return carry
 
-    lax.fori_loop(0, 8, first_pass, 0)
-    arrived("ylb", "yrb", "xlb", "xrb")
+    lax.fori_loop(0, 4, first_pass, 0)
+    arrived("ylb", "yrb")
+    lax.fori_loop(4, 8, first_pass, 0)
+    arrived("ylc", "yrc")
     corners()
     pl.semaphore_wait(rounds.at[1], len(second_round))
     greet(rounds.at[2], third_round)
@@ -262,18 +316,45 @@
     def product(a, b):
         return lax.dot_general(a, b, (((1,), (1,)), ((), ())), preferred_element_type=F32)
 
-    acc[...] = jnp.zeros_like(acc)
-
-    def multiply(t, carry):
+    arrived("hyl", "hyr", "hxl", "hxr", "cyl", "cyr", "cxl", "cxr")
+    sums = None
+    for t in range(4):
         a, b, c, d = (
-            jnp.concatenate([ref[t, k] for k in range(16)], axis=1) for ref in (lh, ll, rh, rl)
+            jnp.concatenate([ref[t, k, half, 0:256, :] for k in range(16)], axis=1)
+            for ref, half in ((lf, 0), (lf, 1), (rf, 0), (rf, 1))
         )
-        acc[...] += product(a, c) + product(a, d) + product(b, c)
-        return carry
-
-    lax.fori_loop(0, 4, multiply, 0)
+        part = product(a, c) + product(a, d) + product(b, c)
+        sums = part if sums is None else sums + part
+
+    xpack = pack(lambda c: ext[(8 if c // 4 < 2 else 0) + c // 4, 4 + c % 4])
+    edges(4, xpack, jnp.where(lane32 < 64, hxr[...], hxl[...]))
+    ypack = pack(lambda c: ext[4 + c // 4, (8 if c % 4 < 2 else 0) + c % 4])
+    edges(8, ypack, jnp.where(lane32 % 32 < 16, hyr[...], hyl[...]))
+    halo = hpk[...]
+    for k, s in enumerate(SHIFTS):
+        side_x, side_y = (hxr, hyr) if s > 0 else (hxl, hyl)
+        inside_x = lane32 < 128 - 32 * s if s > 0 else lane32 >= -32 * s
+        inside_y = lane32 % 32 < 32 - 8 * s if s > 0 else lane32 % 32 >= -8 * s
+        epk[13 + k] = jnp.where(inside_x, rolled(halo, -32 * s), rolled(side_x[...], -32 * s))
+        over = 32 - 8 * s if s > 0 else -32 - 8 * s
+        epk[17 + k] = jnp.where(inside_y, rolled(halo, -8 * s), rolled(side_y[...], over))
+
+    eights = jnp.where(lax.broadcasted_iota(jnp.int32, (32, 128), 0) < 16, 1.0, 8.0)
+    halo_columns = [(x, y) for x in (-2, -1, 4, 5) for y in range(4)]
+    for m, (x, y) in enumerate(halo_columns):
+        c = (x % 4) * 4 + y % 4
+        for k, s in enumerate(SHIFTS):
+            value = ext[4 + x, 4 + y]
+            edge = rolled(epk[4 + k], 124 - 8 * c)
+            value = jnp.where(rim32, edge, rolled(value, -s))
+            shifted[m, k] = value * eights if k < 2 else value
+
+    for k in range(4):
+        for r in range(8):
+            for side, ref in enumerate((cxl, cxr, cyl, cyr)):
+                halo_coef[k, side, r] = jnp.broadcast_to(ref[k, r : r + 1, :], (8, 128))
     for k in range(ngx):
-        cas[k] = acc[nb * k : nb * (k + 1), :] * scale
+        cas[k] = sums[nb * k : nb * (k + 1), :] * scale
 
     pl.semaphore_wait(rounds.at[2], len(third_round))
     first = []
@@ -307,20 +388,9 @@
         for copy in second:
             copy.start()
 
-    arrived("xlf", "xrf", "ylf", "yrf", "hyl", "hyr", "hxl", "hxr", "cyl", "cyr", "cxl", "cxr")
+    arrived("xlf", "xrf", "ylf", "yrf")
     arrived("cll", "clr", "crl", "crr")
-    xpack = pack(lambda c: ext[(8 if c // 4 < 2 else 0) + c // 4, 4 + c % 4])
-    edges(4, xpack, jnp.where(lane32 < 64, hxr[...], hxl[...]))
-    ypack = pack(lambda c: ext[4 + c // 4, (8 if c % 4 < 2 else 0) + c % 4])
-    edges(8, ypack, jnp.where(lane32 % 32 < 16, hyr[...], hyl[...]))
-    halo = hpk[...]
-    for k, s in enumerate(SHIFTS):
-        side_x, side_y = (hxr, hyr) if s > 0 else (hxl, hyl)
-        inside_x = lane32 < 128 - 32 * s if s > 0 else lane32 >= -32 * s
-        inside_y = lane32 % 32 < 32 - 8 * s if s > 0 else lane32 % 32 >= -8 * s
-        epk[13 + k] = jnp.where(inside_x, rolled(halo, -32 * s), rolled(side_x[...], -32 * s))
-        over = 32 - 8 * s if s > 0 else -32 - 8 * s
-        epk[17 + k] = jnp.where(inside_y, rolled(halo, -8 * s), rolled(side_y[...], over))
+    inner16 = lane16 % 8 < 4
 
     def second_pass(i, carry):
         def at(x, y):
@@ -328,13 +398,16 @@
                 return nall[i, x + 2, y + 2]
             return nbuf[x + 4, y + 4]
 
-        rims = {4: packed_slope(i, 4), 8: packed_slope(i, 8)}
         zedge = (
             wide(czh[0:1, :]) * packed(i, 12)
             + wide(czh[1:2, :]) * packed_slope(i, 13)
             + wide(czh[2:3, :]) * packed_slope(i, 17)
             + wide(czh[3:4, :]) * packed_slope(i, 21)
         )
+        rims = packed_slope(i, 8)
+        high = jnp.where(inner16, fzp[i], zedge)
+        low = jnp.where(inner16, zedge, fzp[i])
+        zends = stencil(*(jnp.where(inner16, rolled(high, -s), rolled(low, -s)) for s in SHIFTS))
         for x in (-4, -3, -2, -1, 0, 1, 2, 3, 4, 5, 6, 7):
             if 0 <= x < 4:
                 ys = (-4, -3, 6, 7)
@@ -345,39 +418,39 @@
             for y in ys:
                 nbuf[4 + x, 4 + y] = density(i, x, y)
 
-        def halo_flux(x, y, refs, row, at_pack):
+        def halo_flux(x, y, side, row, sz):
             n = at(x, y)
             sx = stencil(*(at(x + s, y) for s in SHIFTS))
             sy = stencil(*(at(x, y + s) for s in SHIFTS))
-            sz = slope_z(n, rims[at_pack], (x % 4) * 4 + y % 4)
-            c0, c1, c2, c3 = (wide(refs[k, row : row + 1, :]) for k in range(4))
+            c0, c1, c2, c3 = (twice(halo_coef[k, side, row]) for k in range(4))
             return c0 * n + c1 * sx + c2 * sy + c3 * sz
 
         for x in (-2, -1, 4, 5):
             for y in range(4):
-                refs, row = (cxl, (x + 2) * 4 + y) if x < 0 else (cxr, (x - 4) * 4 + y)
-                fxb[i, x + 2, y] = halo_flux(x, y, refs, row, 4)
+                m = halo_columns.index((x, y))
+                moved = [wide(shifted[m, k, pl.ds(i, 1), :]) * shifted[m, k, 16:32, :] for k in range(4)]
+                sz = (moved[0] - moved[1]) - (moved[2] - moved[3])
+                side, row = (0, (x + 2) * 4 + y) if x < 0 else (1, (x - 4) * 4 + y)
+                fxb[i, x + 2, y] = halo_flux(x, y, side, row, sz)
         for x in range(4):
             for y in (-2, -1, 4, 5):
-                refs, row = (cyl, x * 2 + y + 2) if y < 0 else (cyr, x * 2 + y - 4)
-                fyb[i, x, y + 2] = halo_flux(x, y, refs, row, 8)
+                sz = slope_z(at(x, y), rims, 4 * x + y % 4)
+                side, row = (2, x * 2 + y + 2) if y < 0 else (3, x * 2 + y - 4)
+                fyb[i, x, y + 2] = halo_flux(x, y, side, row, sz)
 
         for c in range(16):
             x, y = divmod(c, 4)
             dx = stencil(*(fxb[i, x + 2 + s, y] for s in SHIFTS))
             dy = stencil(*(fyb[i, x, y + 2 + s] for s in SHIFTS))
             flux = fzb[i, c]
-            near = []
-            for s in SHIFTS:
-                beyond = lane16 >= 128 - s if s > 0 else lane16 < -s
-                near.append(jnp.where(beyond, rolled(zedge, 124 - s - 8 * c), rolled(flux, -s)))
-            dz = stencil(*near)
+            dz = stencil(*(rolled(flux, -s) for s in SHIFTS))
+            dz = jnp.where(rim, rolled(zends, 124 - 8 * c), dz)
             pot[pl.ds(i * 256 + c, 16, stride=16), :] = local_pot[i, c] - (dx + dy + dz)
         return carry
 
-    lax.fori_loop(0, 6, second_pass, 0)
+    lax.fori_loop(0, 9, second_pass, 0)
     reduce_first()
-    lax.fori_loop(6, 16, second_pass, 0)
+    lax.fori_loop(9, 16, second_pass, 0)
 
     for copy in second:
         copy.wait_recv()
@@ -395,7 +468,7 @@
     vmem = pltpu.VMEM
     dma = pltpu.SemaphoreType.DMA
     scratch = [
-        vmem((12, 12, 32, 128), F32), vmem((7, 16, 128), F32),
+        vmem((12, 12, 32, 128), F32), vmem((7, 16, 8, 128), F32),
         vmem((4, 16, 128), F32), vmem((4, 8, 128), F32), vmem((4, 8, 128), F32),
         vmem((4, 16, 128), F32), vmem((4, 8, 128), F32), vmem((4, 8, 128), F32),
         vmem((4, 8, 128), F32), vmem((4, 8, 128), F32),
@@ -404,13 +477,14 @@
         vmem((32, 128), F32), vmem((32, 128), F32), vmem((8, 128), F32),
         vmem((25, 32, 128), F32),
         vmem((16, 8, 8, 16, 128), F32), vmem((12, 12, 16, 128), F32),
+        vmem((16, 16, 16, 128), F32), vmem((16, 16, 16, 128), F32), vmem((16, 16, 128), F32),
+        vmem((16, 4, 32, 128), F32), vmem((4, 4, 8, 8, 128), F32),
         vmem((16, 8, 4, 16, 128), F32), vmem((16, 4, 8, 16, 128), F32), vmem((16, 16, 16, 128), F32),
         vmem((16, 16, 16, 128), F32),
-        vmem((4, 16, 256, 128), BF16), vmem((4, 16, 256, 128), BF16),
-        vmem((4, 16, 256, 128), BF16), vmem((4, 16, 256, 128), BF16), vmem((256, 256), F32),
+        vmem((4, 16, 2, 272, 128), BF16), vmem((4, 16, 2, 272, 128), BF16),
         vmem((ngx, nb, 256), F32), vmem((ngx, nb, 256), F32),
         vmem((nb, 1, 256), F32), vmem((nb, 1, 256), F32),
-        dma((32,)), dma((32,)), dma((ngx,)), dma((ngx,)), dma((nb,)), dma((nb,)),
+        dma((36,)), dma((36,)), dma((ngx,)), dma((ngx,)), dma((nb,)), dma((nb,)),
         pltpu.SemaphoreType.REGULAR((3,)),
     ]
     inner = pl.BlockSpec(memory_space=pltpu.VMEM)
@@ -424,7 +498,7 @@
         out_specs=(inner, inner),
         scratch_shapes=scratch,
         compiler_params=pltpu.CompilerParams(
-            collective_id=0, has_side_effects=True, vmem_limit_bytes=44 * 1024 * 1024
+            collective_id=0, has_side_effects=True, vmem_limit_bytes=50 * 1024 * 1024
         ),
     )(jnp.concatenate([occupied, virtual, kernel_fields, density_grad], axis=0).reshape(624, 128))
     return potential.reshape(256, 4, 4, 128), row

time: 47.4 us -> 44.2 us (0.932)
  Pallas kernels: 43.7 us -> 40.5 us
    pallas_call x1, Pallas kernels: 43.7 us -> 40.5 us  [on_device(): pl.pallas_call(functools.partial(kernel, sizes, scale), out_shape=(jax.Sh...]
where the time goes in v4:
time: 44.2 us; the launch traced here: 44.1 us
  Pallas kernels  40.5 us (92%)
  local copies, waits for them, and re-layouts  1.88 us (4%)
  other arithmetic  1.08 us (2%)
  between operations  0.64 us (1%)
    pallas_call x1, Pallas kernels, on_device(): pl.pallas_call(functools.partial(kernel, sizes, scale), out_shape=(jax.Sh...  40.5 us
    unnamed x2, local copies, waits for them, and re-layouts  1.88 us
    concatenate x1, other arithmetic, on_device(): jnp.concatenate([occupied, virtual, kernel_fields, density_grad], axis=0)  1.08 us

profile of v4, /device:TPU:1, one launch (start us, length us, event | category | flops | bytes accessed | tf_op | source)
XLA Modules:
  0.0 44.1 jit_solution(6495799969726095739)
XLA Ops:
  0.6 1.1 %pad_maximum_fusion = f32[39,4,4,128]{3,2,1,0:T(4,128)S(1)} fusion(f32[3,4,4,128]{3,2,1,0:T(4,128)} %param.7, f32[4,4,4,128]{3,2,1,0:T(4,128)} %param.6, f32[16,4,4,128]{3,2,1,0:T(4,128)} %param.5, f32[16,4,4,128]{3,2,1,0:T(4,128)} %param.4), kind=kLoop, calls=%fused_computation | loop fusion | flops 239616 | bytes 638976 | tf_op jit(solution)/shard_map/concatenate | solution.py:503
  1.7 40.5 %shard_map.59 = (f32[4096,128]{1,0:T(8,128)S(1)}, f32[1,256]{1,0:T(1,128)S(1)}) custom-call(f32[624,128]{1,0:T(8,128)S(1)} %bitcast.3), custom_call_target="tpu_custom_call" | custom-call | tf_op jit(solution)/shard_map/pallas_call | solution.py:491
  42.2 1.3 %copy.8 = f32[256,4,4,128]{3,2,1,0:T(4,128)} copy(f32[256,4,4,128]{3,2,1,0:T(4,128)S(1)} %bitcast.2) | data formatting | bytes 4194304
  43.5 0.6 %copy.9 = f32[1,256]{1,0:T(1,128)} copy(f32[1,256]{1,0:T(1,128)S(1)} %get-tuple-element.9) | data formatting | bytes 2048

commit v5 on v4

--- a/solution.py
+++ b/solution.py
@@ -41,7 +41,7 @@
     pot, cas_out,
     ext, own, cxo, cxl, cxr, cyo, cyhi, cylo, cyl, cyr,
     opk, zl, zr, hpk, hxl, hxr, hyl, hyr, czh, epk,
-    nall, nbuf, sxb, szb, fzp, shifted, halo_coef, fxb, fyb, fzb, local_pot, lf, rf,
+    nall, nbuf, szb, fzp, shifted, halo_coef, fxb, fyb, fzb, local_pot, lf, rf, ly, ry, acc,
     cas, ra, dbuf, rb,
     send, recv, asend, arecv, bsend, brecv, rounds,
 ):
@@ -77,7 +77,8 @@
     f0, f1, f2, f3 = (everything[pl.ds(512 + 16 * k, 16), :] for k in range(4))
     g = [everything[pl.ds(576 + 16 * k, 16), :] * (1.0 / 12.0) for k in range(3)]
     f3s = f3 * (1.0 / 144.0)
-    for k, value in enumerate((f0, f1, f2, f3s, *g)):
+    crossed = (g[0] * g[1] * f2, g[1] * g[1] * f2 + f3s, g[2] * g[1] * f2, g[1] * f1)
+    for k, value in enumerate((f0, f1, f2, f3s, *g, *crossed)):
         for c in range(16):
             own[k, c] = jnp.broadcast_to(value[c : c + 1, :], (8, 128))
 
@@ -186,6 +187,9 @@
         sz = stencil(*(rolled(n, -s) for s in SHIFTS))
         return jnp.where(rim, rolled(rims, 124 - 8 * c), sz)
 
+    def keep(factors, at, rows, value):
+        factors[at, 0, rows, :], factors[at, 1, rows, :] = split_halves(value)
+
     def own_columns(i, carry):
         rows = rows_of(i)
         for c in range(16):
@@ -193,7 +197,7 @@
             n = density(i, x, y)
             nall[i, x + 2, y + 2] = n
             szb[i, c] = stencil(*(rolled(n, -s) for s in SHIFTS))
-            lf[0, c, 0, rows, :], lf[0, c, 1, rows, :] = split_halves(n)
+            keep(lf, c, rows, n)
         return carry
 
     lax.fori_loop(0, 16, own_columns, 0)
@@ -208,20 +212,8 @@
         low = jnp.where(inner32, hpack, opack)
         for k, s in enumerate(SHIFTS):
             epk[at + k] = jnp.where(inner32, rolled(high, -s), rolled(low, -s))
-        return high, low
-
-    halo = hpk[...]
-    high, low = edges(0, opk[0:32, :], halo)
-    for k, s in enumerate(SHIFTS):
-        epk[21 + k] = jnp.where(inner32, rolled(low, -s), rolled(high, -s))
-    epk[12] = halo
-
-    push("hyl", hpk, hyl, device(dy=1))
-    push("hyr", hpk, hyr, device(dy=-1))
-    push("hxl", hpk, hxl, device(dx=1))
-    push("hxr", hpk, hxr, device(dx=-1))
-    push_y("f")
-    push_x("f")
+
+    edges(0, opk[0:32, :], hpk[...])
 
     def corners():
         for name, src, dst, target in (
@@ -250,26 +242,31 @@
                 c = 4 * x + y
                 sx = stencil(*(line[x + s] for s in SHIFTS))
                 sz = jnp.where(rim, rolled(rims, 124 - 8 * c), szb[i, c])
-                g0, g2 = coefficients(c, (4, 6))
-                sxb[i, c] = sx
-                szb[i, c] = sz
-                local_pot[i, c] = g0 * sx + g2 * sz
-                for term, value in ((1, sx), (3, sz)):
-                    lf[term, c, 0, rows, :], lf[term, c, 1, rows, :] = split_halves(value)
+                n = line[x]
+                f0, f1, f2, f3, g0, g1, g2 = coefficients(c, range(7))
+                aligned = g0 * sx + g2 * sz
+                scalar = f1 * n + f2 * aligned
+                values = (f0 * n + f1 * aligned, g0 * scalar + f3 * sx, g2 * scalar + f3 * sz)
+                local_pot[i, c], fxb[i, x + 2, y], fzb[i, c] = values
+                fyb[i, x, y + 2] = g1 * scalar
+                for term, value in enumerate(values):
+                    keep(rf, 16 * term + c, rows, value)
+                for term, value in ((1, sx), (2, sz), (3, g1 * scalar)):
+                    keep(lf, 16 * term + c, rows, value)
         return carry
 
     arrived("xlv", "xrv", "xla", "xra", "xlb", "xrb", "xlc", "xrc")
     lax.fori_loop(0, 16, slopes_xz, 0)
+    push("hyl", hpk, hyl, device(dy=1))
+    push("hyr", hpk, hyr, device(dy=-1))
+    push("hxl", hpk, hxl, device(dx=1))
+    push("hxr", hpk, hxr, device(dx=-1))
     pl.semaphore_wait(rounds.at[0], len(nearest))
     greet(rounds.at[1], second_round)
     arrived("ylv", "yrv", "yla", "yra")
 
-    def first_pass(i, carry):
+    def with_sy(i):
         rows = rows_of(i)
-
-        def keep(term, c, right):
-            rf[term, c, 0, rows, :], rf[term, c, 1, rows, :] = split_halves(right)
-
         ends = None
         for x in range(4):
             line = {}
@@ -280,57 +277,64 @@
                     line[y] = density(i, x, y)
                     nall[i, x + 2, y + 2] = line[y]
             for y in range(4):
-                n = line[y]
                 c = 4 * x + y
                 sy = stencil(*(line[y + s] for s in SHIFTS))
-                lf[2, c, 0, rows, :], lf[2, c, 1, rows, :] = split_halves(sy)
-                f0, f1, f2, f3, g0, g1, g2 = coefficients(c, range(7))
-                aligned = local_pot[i, c] + g1 * sy
-                scalar = f1 * n + f2 * aligned
-                flux = scalar * g0 + f3 * sxb[i, c]
-                fxb[i, x + 2, y] = flux
-                keep(1, c, flux)
-                flux = scalar * g1 + f3 * sy
+                keep(ly, c, rows, sy)
+                e0, e1, e2, e3 = coefficients(c, range(7, 11))
+                fxb[i, x + 2, y] += e0 * sy
+                flux = fyb[i, x, y + 2] + e1 * sy
                 fyb[i, x, y + 2] = flux
-                keep(2, c, flux)
-                flux = scalar * g2 + f3 * szb[i, c]
+                keep(ry, c, rows, flux)
+                flux = fzb[i, c] + e2 * sy
                 fzb[i, c] = flux
-                keep(3, c, flux)
                 part = rolled(flux, 4 + 8 * c)
                 ends = part if ends is None else jnp.where(lane16 // 8 == c, part, ends)
-                local = f0 * n + f1 * aligned
-                local_pot[i, c] = local
-                keep(0, c, local)
+                local_pot[i, c] += e3 * sy
         fzp[i] = ends
+
+    def product(a, b):
+        return lax.dot_general(a, b, (((1,), (1,)), ((), ())), preferred_element_type=F32)
+
+    def product_of(left, left_at, right, right_at, count):
+        a, b, c, d = (
+            jnp.concatenate([ref[at + k, half, 0:256, :] for k in range(count)], axis=1)
+            for ref, at in ((left, left_at), (right, right_at))
+            for half in range(2)
+        )
+        return product(a, c) + product(a, d) + product(b, c)
+
+    def first_pass(j, carry):
+        acc[...] += product_of(lf, 6 * j, rf, 6 * j, 6)
+        with_sy(2 * j)
+        with_sy(2 * j + 1)
         return carry
 
-    lax.fori_loop(0, 4, first_pass, 0)
+    acc[...] = jnp.zeros_like(acc)
+    lax.fori_loop(0, 2, first_pass, 0)
     arrived("ylb", "yrb")
-    lax.fori_loop(4, 8, first_pass, 0)
+    lax.fori_loop(2, 4, first_pass, 0)
     arrived("ylc", "yrc")
+    push_y("f")
+    push_x("f")
     corners()
     pl.semaphore_wait(rounds.at[1], len(second_round))
     greet(rounds.at[2], third_round)
-    lax.fori_loop(8, 16, first_pass, 0)
-
-    def product(a, b):
-        return lax.dot_general(a, b, (((1,), (1,)), ((), ())), preferred_element_type=F32)
+    lax.fori_loop(4, 8, first_pass, 0)
 
     arrived("hyl", "hyr", "hxl", "hxr", "cyl", "cyr", "cxl", "cxr")
-    sums = None
-    for t in range(4):
-        a, b, c, d = (
-            jnp.concatenate([ref[t, k, half, 0:256, :] for k in range(16)], axis=1)
-            for ref, half in ((lf, 0), (lf, 1), (rf, 0), (rf, 1))
-        )
-        part = product(a, c) + product(a, d) + product(b, c)
-        sums = part if sums is None else sums + part
+    sums = acc[...] + product_of(ly, 0, ry, 0, 16) + product_of(lf, 48, ly, 0, 16)
 
     xpack = pack(lambda c: ext[(8 if c // 4 < 2 else 0) + c // 4, 4 + c % 4])
     edges(4, xpack, jnp.where(lane32 < 64, hxr[...], hxl[...]))
     ypack = pack(lambda c: ext[4 + c // 4, (8 if c % 4 < 2 else 0) + c % 4])
     edges(8, ypack, jnp.where(lane32 % 32 < 16, hyr[...], hyl[...]))
     halo = hpk[...]
+    high = jnp.where(inner32, opk[0:32, :], halo)
+    low = jnp.where(inner32, halo, opk[0:32, :])
+    for k, s in enumerate(SHIFTS):
+        epk[21 + k] = jnp.where(inner32, rolled(low, -s), rolled(high, -s))
+    epk[12] = halo
+
     for k, s in enumerate(SHIFTS):
         side_x, side_y = (hxr, hyr) if s > 0 else (hxl, hyl)
         inside_x = lane32 < 128 - 32 * s if s > 0 else lane32 >= -32 * s
@@ -358,7 +362,7 @@
 
     pl.semaphore_wait(rounds.at[2], len(third_round))
     first = []
-    for k in range(1, ngx):
+    for k in sorted(range(1, ngx), key=lambda k: -min(k, ngx - k)):
         copy = pltpu.make_async_remote_copy(
             src_ref=cas.at[lax.rem(gx + k, ngx)], dst_ref=ra.at[k],
             send_sem=asend.at[k], recv_sem=arecv.at[k],
@@ -367,7 +371,12 @@
         copy.start()
         first.append(copy)
     second = []
-    for k in range(1, nb):
+
+    def hops(k):
+        dy, dz = k // ngz, k % ngz
+        return 2 * min(dy, ngy - dy) + min(dz, ngz - dz)
+
+    for k in sorted(range(1, nb), key=lambda k: -hops(k)):
         there = device(dy=k // ngz, dz=k % ngz)
         second.append(
             pltpu.make_async_remote_copy(
@@ -448,9 +457,9 @@
             pot[pl.ds(i * 256 + c, 16, stride=16), :] = local_pot[i, c] - (dx + dy + dz)
         return carry
 
-    lax.fori_loop(0, 9, second_pass, 0)
+    lax.fori_loop(0, 8, second_pass, 0)
     reduce_first()
-    lax.fori_loop(9, 16, second_pass, 0)
+    lax.fori_loop(8, 16, second_pass, 0)
 
     for copy in second:
         copy.wait_recv()
@@ -468,7 +477,7 @@
     vmem = pltpu.VMEM
     dma = pltpu.SemaphoreType.DMA
     scratch = [
-        vmem((12, 12, 32, 128), F32), vmem((7, 16, 8, 128), F32),
+        vmem((12, 12, 32, 128), F32), vmem((11, 16, 8, 128), F32),
         vmem((4, 16, 128), F32), vmem((4, 8, 128), F32), vmem((4, 8, 128), F32),
         vmem((4, 16, 128), F32), vmem((4, 8, 128), F32), vmem((4, 8, 128), F32),
         vmem((4, 8, 128), F32), vmem((4, 8, 128), F32),
@@ -477,11 +486,12 @@
         vmem((32, 128), F32), vmem((32, 128), F32), vmem((8, 128), F32),
         vmem((25, 32, 128), F32),
         vmem((16, 8, 8, 16, 128), F32), vmem((12, 12, 16, 128), F32),
-        vmem((16, 16, 16, 128), F32), vmem((16, 16, 16, 128), F32), vmem((16, 16, 128), F32),
+        vmem((16, 16, 16, 128), F32), vmem((16, 16, 128), F32),
         vmem((16, 4, 32, 128), F32), vmem((4, 4, 8, 8, 128), F32),
         vmem((16, 8, 4, 16, 128), F32), vmem((16, 4, 8, 16, 128), F32), vmem((16, 16, 16, 128), F32),
         vmem((16, 16, 16, 128), F32),
-        vmem((4, 16, 2, 272, 128), BF16), vmem((4, 16, 2, 272, 128), BF16),
+        vmem((64, 2, 272, 128), BF16), vmem((48, 2, 272, 128), BF16),
+        vmem((16, 2, 272, 128), BF16), vmem((16, 2, 272, 128), BF16), vmem((256, 256), F32),
         vmem((ngx, nb, 256), F32), vmem((ngx, nb, 256), F32),
         vmem((nb, 1, 256), F32), vmem((nb, 1, 256), F32),
         dma((36,)), dma((36,)), dma((ngx,)), dma((ngx,)), dma((nb,)), dma((nb,)),

time: 44.2 us -> 42.7 us (0.966)
  Pallas kernels: 40.5 us -> 39 us
    pallas_call x1, Pallas kernels: 40.5 us -> 39 us  [on_device(): pl.pallas_call(functools.partial(kernel, sizes, scale), out_shape=(jax.Sh...]
where the time goes in v5:
time: 42.7 us; the launch traced here: 42.6 us
  Pallas kernels  39 us (91%)
  local copies, waits for them, and re-layouts  1.88 us (4%)
  other arithmetic  1.08 us (3%)
  between operations  0.64 us (1%)
    pallas_call x1, Pallas kernels, on_device(): pl.pallas_call(functools.partial(kernel, sizes, scale), out_shape=(jax.Sh...  39 us
    unnamed x2, local copies, waits for them, and re-layouts  1.88 us
    concatenate x1, other arithmetic, on_device(): jnp.concatenate([occupied, virtual, kernel_fields, density_grad], axis=0)  1.08 us

profile of v5, /device:TPU:1, one launch (start us, length us, event | category | flops | bytes accessed | tf_op | source)
XLA Modules:
  0.0 42.6 jit_solution(3836186745861393014)
XLA Ops:
  0.6 1.1 %pad_maximum_fusion = f32[39,4,4,128]{3,2,1,0:T(4,128)S(1)} fusion(f32[3,4,4,128]{3,2,1,0:T(4,128)} %param.7, f32[4,4,4,128]{3,2,1,0:T(4,128)} %param.6, f32[16,4,4,128]{3,2,1,0:T(4,128)} %param.5, f32[16,4,4,128]{3,2,1,0:T(4,128)} %param.4), kind=kLoop, calls=%fused_computation | loop fusion | flops 239616 | bytes 638976 | tf_op jit(solution)/shard_map/concatenate | solution.py:513
  1.7 39.0 %shard_map.59 = (f32[4096,128]{1,0:T(8,128)S(1)}, f32[1,256]{1,0:T(1,128)S(1)}) custom-call(f32[624,128]{1,0:T(8,128)S(1)} %bitcast.3), custom_call_target="tpu_custom_call" | custom-call | tf_op jit(solution)/shard_map/pallas_call | solution.py:501
  40.7 1.3 %copy.8 = f32[256,4,4,128]{3,2,1,0:T(4,128)} copy(f32[256,4,4,128]{3,2,1,0:T(4,128)S(1)} %bitcast.2) | data formatting | bytes 4194304
  42.1 0.6 %copy.9 = f32[1,256]{1,0:T(1,128)} copy(f32[1,256]{1,0:T(1,128)S(1)} %get-tuple-element.9) | data formatting | bytes 2048

commit v6 on v5

--- a/solution.py
+++ b/solution.py
@@ -203,6 +203,8 @@
     lax.fori_loop(0, 16, own_columns, 0)
 
     arrived("zl", "zr")
+    pl.semaphore_wait(rounds.at[0], len(nearest))
+    greet(rounds.at[1], second_round)
     inner32 = lane32 % 8 < 4
     hpk[...] = jnp.where(inner32, zl[0:32, :], zr[0:32, :])
     czh[...] = jnp.where(lanes(8) % 8 < 4, zl[32:40, :], zr[32:40, :])
@@ -215,14 +217,15 @@
 
     edges(0, opk[0:32, :], hpk[...])
 
-    def corners():
-        for name, src, dst, target in (
-            ("cll", ext.at[up, pl.ds(2, 2)], ext.at[pl.ds(2, 2), pl.ds(2, 2)], 1),
-            ("clr", ext.at[up, pl.ds(8, 2)], ext.at[pl.ds(2, 2), pl.ds(8, 2)], 1),
-            ("crl", ext.at[down, pl.ds(2, 2)], ext.at[pl.ds(8, 2), pl.ds(2, 2)], -1),
-            ("crr", ext.at[down, pl.ds(8, 2)], ext.at[pl.ds(8, 2), pl.ds(8, 2)], -1),
+    def corners(tag, rows):
+        for name, src, src_y, dst, dst_y, target in (
+            ("cll", up, 2, 2, 2, 1), ("clr", up, 8, 2, 8, 1),
+            ("crl", down, 2, 8, 2, -1), ("crr", down, 8, 8, 8, -1),
         ):
-            push(name, src, dst, device(dx=target))
+            push(
+                name + tag, ext.at[src, pl.ds(src_y, 2), rows],
+                ext.at[pl.ds(dst, 2), pl.ds(dst_y, 2), rows], device(dx=target),
+            )
 
     def coefficients(c, which):
         return (twice(own[k, c]) for k in which)
@@ -257,13 +260,13 @@
 
     arrived("xlv", "xrv", "xla", "xra", "xlb", "xrb", "xlc", "xrc")
     lax.fori_loop(0, 16, slopes_xz, 0)
+    push_x("f")
     push("hyl", hpk, hyl, device(dy=1))
     push("hyr", hpk, hyr, device(dy=-1))
     push("hxl", hpk, hxl, device(dx=1))
     push("hxr", hpk, hxr, device(dx=-1))
-    pl.semaphore_wait(rounds.at[0], len(nearest))
-    greet(rounds.at[1], second_round)
     arrived("ylv", "yrv", "yla", "yra")
+    corners("v", pl.ds(16, 16))
 
     def with_sy(i):
         rows = rows_of(i)
@@ -312,14 +315,13 @@
     acc[...] = jnp.zeros_like(acc)
     lax.fori_loop(0, 2, first_pass, 0)
     arrived("ylb", "yrb")
+    push_y("f")
     lax.fori_loop(2, 4, first_pass, 0)
     arrived("ylc", "yrc")
-    push_y("f")
-    push_x("f")
-    corners()
+    corners("o", pl.ds(0, 16))
+    lax.fori_loop(4, 8, first_pass, 0)
     pl.semaphore_wait(rounds.at[1], len(second_round))
     greet(rounds.at[2], third_round)
-    lax.fori_loop(4, 8, first_pass, 0)
 
     arrived("hyl", "hyr", "hxl", "hxr", "cyl", "cyr", "cxl", "cxr")
     sums = acc[...] + product_of(ly, 0, ry, 0, 16) + product_of(lf, 48, ly, 0, 16)
@@ -360,7 +362,6 @@
     for k in range(ngx):
         cas[k] = sums[nb * k : nb * (k + 1), :] * scale
 
-    pl.semaphore_wait(rounds.at[2], len(third_round))
     first = []
     for k in sorted(range(1, ngx), key=lambda k: -min(k, ngx - k)):
         copy = pltpu.make_async_remote_copy(
@@ -394,11 +395,12 @@
             part = part + ra[k]
         for r in range(nb):
             dbuf[r] = part[r : r + 1, :]
+        pl.semaphore_wait(rounds.at[2], len(third_round))
         for copy in second:
             copy.start()
 
     arrived("xlf", "xrf", "ylf", "yrf")
-    arrived("cll", "clr", "crl", "crr")
+    arrived("cllv", "clrv", "crlv", "crrv", "cllo", "clro", "crlo", "crro")
     inner16 = lane16 % 8 < 4
 
     def second_pass(i, carry):
@@ -494,7 +496,7 @@
         vmem((16, 2, 272, 128), BF16), vmem((16, 2, 272, 128), BF16), vmem((256, 256), F32),
         vmem((ngx, nb, 256), F32), vmem((ngx, nb, 256), F32),
         vmem((nb, 1, 256), F32), vmem((nb, 1, 256), F32),
-        dma((36,)), dma((36,)), dma((ngx,)), dma((ngx,)), dma((nb,)), dma((nb,)),
+        dma((40,)), dma((40,)), dma((ngx,)), dma((ngx,)), dma((nb,)), dma((nb,)),
         pltpu.SemaphoreType.REGULAR((3,)),
     ]
     inner = pl.BlockSpec(memory_space=pltpu.VMEM)

time: 42.7 us -> 41.9 us (0.981)
  Pallas kernels: 39 us -> 38.2 us
    pallas_call x1, Pallas kernels: 39 us -> 38.2 us  [on_device(): pl.pallas_call(functools.partial(kernel, sizes, scale), out_shape=(jax.Sh...]
where the time goes in v6:
time: 41.9 us; the launch traced here: 41.8 us
  Pallas kernels  38.2 us (91%)
  local copies, waits for them, and re-layouts  1.88 us (4%)
  other arithmetic  1.08 us (3%)
  between operations  0.64 us (2%)
    pallas_call x1, Pallas kernels, on_device(): pl.pallas_call(functools.partial(kernel, sizes, scale), out_shape=(jax.Sh...  38.2 us
    unnamed x2, local copies, waits for them, and re-layouts  1.88 us
    concatenate x1, other arithmetic, on_device(): jnp.concatenate([occupied, virtual, kernel_fields, density_grad], axis=0)  1.08 us

profile of v6, /device:TPU:1, one launch (start us, length us, event | category | flops | bytes accessed | tf_op | source)
XLA Modules:
  0.0 41.8 jit_solution(10667466447701484925)
XLA Ops:
  0.6 1.1 %pad_maximum_fusion = f32[39,4,4,128]{3,2,1,0:T(4,128)S(1)} fusion(f32[3,4,4,128]{3,2,1,0:T(4,128)} %param.7, f32[4,4,4,128]{3,2,1,0:T(4,128)} %param.6, f32[16,4,4,128]{3,2,1,0:T(4,128)} %param.5, f32[16,4,4,128]{3,2,1,0:T(4,128)} %param.4), kind=kLoop, calls=%fused_computation | loop fusion | flops 239616 | bytes 638976 | tf_op jit(solution)/shard_map/concatenate | solution.py:515
  1.7 38.2 %shard_map.59 = (f32[4096,128]{1,0:T(8,128)S(1)}, f32[1,256]{1,0:T(1,128)S(1)}) custom-call(f32[624,128]{1,0:T(8,128)S(1)} %bitcast.3), custom_call_target="tpu_custom_call" | custom-call | tf_op jit(solution)/shard_map/pallas_call | solution.py:503
  40.0 1.3 %copy.8 = f32[256,4,4,128]{3,2,1,0:T(4,128)} copy(f32[256,4,4,128]{3,2,1,0:T(4,128)S(1)} %bitcast.2) | data formatting | bytes 4194304
  41.3 0.6 %copy.9 = f32[1,256]{1,0:T(1,128)} copy(f32[1,256]{1,0:T(1,128)S(1)} %get-tuple-element.9) | data formatting | bytes 2048

commit v7 on v6

--- a/solution.py
+++ b/solution.py
@@ -134,7 +134,7 @@
 
     push("zl", opk, zl, device(dz=1))
     push("zr", opk, zr, device(dz=-1))
-    blocks = {"v": pl.ds(16, 16), "a": pl.ds(0, 4), "b": pl.ds(4, 4), "c": pl.ds(8, 8), "f": pl.ds(0, 32)}
+    blocks = {"v": pl.ds(16, 16), "a": pl.ds(0, 4), "b": pl.ds(4, 4), "c": pl.ds(8, 8), "f": pl.ds(0, 32), "n": pl.ds(0, 32)}
     up, down, four = pl.ds(6, 2), pl.ds(4, 2), pl.ds(4, 4)
 
     def push_y(kind):
@@ -153,9 +153,9 @@
         src, dst = (down, pl.ds(8, 2)) if near else (up, pl.ds(10, 2))
         push("xr" + kind, ext.at[src, four, rows], ext.at[dst, four, rows], device(dx=-1))
 
+    push_x("n")
     for kind in "vabc":
         push_y(kind)
-        push_x(kind)
     push("cyl", cyhi, cyl, device(dy=1))
     push("cyr", cylo, cyr, device(dy=-1))
     push("cxl", cxo.at[:, 8:16], cxl, device(dx=1))
@@ -258,7 +258,7 @@
                     keep(lf, 16 * term + c, rows, value)
         return carry
 
-    arrived("xlv", "xrv", "xla", "xra", "xlb", "xrb", "xlc", "xrc")
+    arrived("xln", "xrn")
     lax.fori_loop(0, 16, slopes_xz, 0)
     push_x("f")
     push("hyl", hpk, hyl, device(dy=1))

time: 41.9 us -> 41.6 us (level)
  no operation moved by 1% of the time
where the time goes in v7:
time: 41.6 us; the launch traced here: 41.5 us
  Pallas kernels  37.9 us (91%)
  local copies, waits for them, and re-layouts  1.88 us (5%)
  other arithmetic  1.08 us (3%)
  between operations  0.64 us (2%)
    pallas_call x1, Pallas kernels, on_device(): pl.pallas_call(functools.partial(kernel, sizes, scale), out_shape=(jax.Sh...  37.9 us
    unnamed x2, local copies, waits for them, and re-layouts  1.88 us
    concatenate x1, other arithmetic, on_device(): jnp.concatenate([occupied, virtual, kernel_fields, density_grad], axis=0)  1.08 us

profile of v7, /device:TPU:1, one launch (start us, length us, event | category | flops | bytes accessed | tf_op | source)
XLA Modules:
  0.0 41.5 jit_solution(8547447247971308098)
XLA Ops:
  0.6 1.1 %pad_maximum_fusion = f32[39,4,4,128]{3,2,1,0:T(4,128)S(1)} fusion(f32[3,4,4,128]{3,2,1,0:T(4,128)} %param.7, f32[4,4,4,128]{3,2,1,0:T(4,128)} %param.6, f32[16,4,4,128]{3,2,1,0:T(4,128)} %param.5, f32[16,4,4,128]{3,2,1,0:T(4,128)} %param.4), kind=kLoop, calls=%fused_computation | loop fusion | flops 239616 | bytes 638976 | tf_op jit(solution)/shard_map/concatenate | solution.py:515
  1.7 37.9 %shard_map.59 = (f32[4096,128]{1,0:T(8,128)S(1)}, f32[1,256]{1,0:T(1,128)S(1)}) custom-call(f32[624,128]{1,0:T(8,128)S(1)} %bitcast.3), custom_call_target="tpu_custom_call" | custom-call | tf_op jit(solution)/shard_map/pallas_call | solution.py:503
  39.7 1.3 %copy.8 = f32[256,4,4,128]{3,2,1,0:T(4,128)} copy(f32[256,4,4,128]{3,2,1,0:T(4,128)S(1)} %bitcast.2) | data formatting | bytes 4194304
  41.0 0.6 %copy.9 = f32[1,256]{1,0:T(1,128)} copy(f32[1,256]{1,0:T(1,128)S(1)} %get-tuple-element.9) | data formatting | bytes 2048
